TPU v7x, 256 devices: a whole 4x4x8 slice. The times are simulated.
256 devices in a mesh: band: 8 (over x, y_lo), grid: 32 (over y_hi, z, core).
Axes of the slice: x: 4, y: 4 (y_hi: 2, y_lo: 2; y = y_hi * 2 + y_lo), z: 8, core: 2. Of those that a mesh axis runs over, the one named last changes fastest.
Arguments:
- wavefunctions: bfloat16 [2048, 524288], P('band', 'grid'), may hold values from -6 to 6
- projectors: bfloat16 [2048, 8, 13, 256], P('grid'), may hold values from -0.0048828125 to 0.0048828125
- slot_atom: int32 [2048, 8], P('grid'), may hold values from -1 to 1023, as said below
- occupations: float32 [2048], P('band'), may hold values from 0.02 to 2
Outputs:
- density: float32 [1024, 13, 13], P('grid')
Inputs may be any that keep to these rules, and one draw needn't show every extreme that they name: `slot_atom`: -1 marks an empty slot. Any other entry is an atom a whose owning domain a // 32 lies within 3 domains, counted around the closed cycle of 32 domains, of the domain of the block, block index // 64. In every domain some block has all 8 slots filled.
All inputs are finite; a program needn't handle non-finite values.
Results may differ from a plain program's by a relative error of at most 0.0003.
Values sent between devices are 32-bit elements; how exact they have to be, the bound alone decides.
No kernel may reach another device: no remote copies, remote signals or barrier semaphores. Data moves between devices by JAX's collectives and lax.ppermute only.
A program may use at most 64 MiB of HBM per device.

v0:
```python
import jax
import jax.numpy as jnp
from jax import lax
from jax.sharding import PartitionSpec as P

REACH = 3
ATOMS_DEV = 32


def shifted(block, axis, distance):
    devices = range(lax.axis_size(axis))
    route = [((i - distance) % len(devices), i) for i in devices]
    return lax.ppermute(block, axis, route)


def from_everyone(x, axis):
    devices = lax.axis_size(axis)
    return lax.all_to_all(jnp.broadcast_to(x[None], (devices, *x.shape)), axis, 0, 0, tiled=True)


def over_copies(x, axis):
    everything = from_everyone(x, axis)
    return jnp.sum(everything, axis=0)


def body(wavefunctions, projectors, slot_atom, occupations):
    band_count = wavefunctions.shape[0]
    block_count, capacity, proj_count, block_len = projectors.shape
    domains = lax.axis_size("grid")
    domain = lax.axis_index("grid")
    window_len = 2 * REACH + 1
    row_len = proj_count * band_count
    grid_blocks = wavefunctions.reshape(band_count, block_count, block_len)
    stacked = projectors.reshape(block_count, capacity * proj_count, block_len)
    slot_terms = jnp.einsum(
        "ngb,gcb->gcn", grid_blocks, stacked, preferred_element_type=jnp.float32
    )
    slot_terms = slot_terms.reshape(block_count * capacity, row_len)
    slot_ids = slot_atom.reshape(-1)
    owner = jnp.floor_divide(slot_ids, ATOMS_DEV)
    offset = jnp.mod(owner - domain + REACH, domains)
    target = jnp.where(
        slot_ids >= 0, offset * ATOMS_DEV + jnp.mod(slot_ids, ATOMS_DEV), window_len * ATOMS_DEV
    )
    selector = (
        jnp.arange(window_len * ATOMS_DEV, dtype=jnp.int32)[:, None] == target[None, :]
    ).astype(jnp.float32)
    window = jnp.dot(
        selector, slot_terms, precision=lax.Precision.HIGHEST, preferred_element_type=jnp.float32
    )
    window = window.reshape(window_len, ATOMS_DEV, row_len)
    forward = window[2 * REACH]
    for hop in range(REACH, 0, -1):
        forward = shifted(forward, "grid", 1) + window[REACH + hop - 1]
    backward = window[0]
    for hop in range(REACH, 0, -1):
        addend = window[REACH - hop + 1] if hop > 1 else jnp.zeros_like(backward)
        backward = shifted(backward, "grid", -1) + addend
    owned = forward + backward
    owned = owned.reshape(ATOMS_DEV, proj_count, band_count)
    weighted = owned * occupations.reshape(1, 1, band_count)
    partial_sum = jnp.einsum("ain,ajn->aij", weighted, owned, precision=lax.Precision.HIGHEST)
    density = over_copies(partial_sum, "band")
    return density


def solution(mesh):
    in_specs = (P("band", "grid"), P("grid", None, None, None), P("grid", None), P("band"))
    out_specs = P("grid", None, None)
    return jax.shard_map(body, mesh=mesh, in_specs=in_specs, out_specs=out_specs, check_vma=False)
```

profile of v0, /device:TPU:8, one launch (start us, length us, event | category | flops | bytes accessed | tf_op | source)
XLA Modules:
  0.0 78.7 jit_solution(8540286206186485369)
XLA Ops:
  0.0 2.8 %copy.11 = bf16[64,8,13,256]{3,0,2,1:T(8,128)(2,1)S(1)} copy(bf16[64,8,13,256]{3,1,2,0:T(8,128)(2,1)} %param.5) | data formatting | bytes 6815744 | tf_op args[1]
  2.8 9.4 %fusion = f32[64,104,256]{2,1,0:T(8,128)} fusion(bf16[32,64,8,256]{3,2,1,0:T(8,128)(2,1)} %bitcast.12, bf16[64,104,256]{2,0,1:T(8,128)(2,1)S(1)} %bitcast.11), kind=kOutput, calls=%fused_computation | convolution fusion | flops 872415232 | bytes 18612224 | tf_op jit(solution)/shard_map/ngb,gcb->gcn/dot_general | solution.py:35
  12.2 8.5 %reshape.104 = f32[512,3328]{1,0:T(8,128)} reshape(f32[64,104,256]{2,1,0:T(8,128)} %fusion) | data formatting | bytes 13631488 | tf_op jit(solution)/shard_map/reshape | solution.py:38
  20.6 0.1 copy.10
  20.7 0.1 reshape.101
  20.8 6.3 %fusion.6 = f32[224,3328]{1,0:T(8,128)S(1)} fusion(f32[512,3328]{1,0:T(8,128)} %reshape.104, s32[512]{0:T(512)S(1)} %fusion.15), kind=kOutput, calls=%fused_computation.7 | convolution fusion | flops 4580294656 | bytes 9799680 | tf_op jit(solution)/shard_map/dot_general | solution.py:48
  27.1 0.1 fusion.17
  27.2 0.1 collective-permute-start
  27.3 0.0 copy-start.1
  27.3 7.1 %collective-permute-start.3 = (f32[32,3328]{1,0:T(8,128)S(1)}, f32[32,3328]{1,0:T(8,128)S(1)}, u32[]{:S(2)}, u32[]{:S(2)}) collective-permute-start(f32[32,3328]{1,0:T(8,128)S(1)} %get-tuple-element.10), channel_id=1, source_target_pairs={{1,0},{2,1},{3,2},{4,3},{5,4},{6,5},{7,6},{8,7},{9,8},{10,9},{11,1... | collective-permute-start | bytes 1277960 | tf_op jit(solution)/shard_map/ppermute | solution.py:13
  34.4 5.7 %collective-permute-done = f32[32,3328]{1,0:T(8,128)S(1)} collective-permute-done((f32[32,3328]{1,0:T(8,128)S(1)}, f32[32,3328]{1,0:T(8,128)S(1)}, u32[]{:S(2)}, u32[]{:S(2)}) %collective-permute-start) | collective-permute-done | bytes 426016 | tf_op jit(solution)/shard_map/ppermute | solution.py:13
  40.1 0.0 collective-permute-done.3
  40.1 0.1 slice_add_fusion.4
  40.2 0.1 collective-permute-start.1
  40.3 5.5 %collective-permute-start.4 = (f32[32,3328]{1,0:T(8,128)S(1)}, f32[32,3328]{1,0:T(8,128)S(1)}, u32[]{:S(2)}, u32[]{:S(2)}) collective-permute-start(f32[32,3328]{1,0:T(8,128)S(1)} %get-tuple-element.8), channel_id=1, source_target_pairs={{1,0},{2,1},{3,2},{4,3},{5,4},{6,5},{7,6},{8,7},{9,8},{10,9},{11,1... | collective-permute-start | bytes 1277960 | tf_op jit(solution)/shard_map/ppermute | solution.py:13
  45.8 5.7 %collective-permute-done.1 = f32[32,3328]{1,0:T(8,128)S(1)} collective-permute-done((f32[32,3328]{1,0:T(8,128)S(1)}, f32[32,3328]{1,0:T(8,128)S(1)}, u32[]{:S(2)}, u32[]{:S(2)}) %collective-permute-start.1) | collective-permute-done | bytes 426016 | tf_op jit(solution)/shard_map/ppermute | solution.py:13
  51.6 0.1 slice_add_fusion.3
  51.7 0.1 collective-permute-start.2
  51.8 5.7 %collective-permute-start.5 = (f32[32,3328]{1,0:T(8,128)S(1)}, f32[32,3328]{1,0:T(8,128)S(1)}, u32[]{:S(2)}, u32[]{:S(2)}) collective-permute-start(f32[32,3328]{1,0:T(8,128)S(1)} %get-tuple-element.6), channel_id=1, source_target_pairs={{1,0},{2,1},{3,2},{4,3},{5,4},{6,5},{7,6},{8,7},{9,8},{10,9},{11,1... | collective-permute-start | bytes 1277960 | tf_op jit(solution)/shard_map/ppermute | solution.py:13
  57.4 5.6 %collective-permute-done.2 = f32[32,3328]{1,0:T(8,128)S(1)} collective-permute-done((f32[32,3328]{1,0:T(8,128)S(1)}, f32[32,3328]{1,0:T(8,128)S(1)}, u32[]{:S(2)}, u32[]{:S(2)}) %collective-permute-start.2) | collective-permute-done | bytes 426016 | tf_op jit(solution)/shard_map/ppermute | solution.py:13
  63.0 0.1 collective-permute-done.5
  63.1 0.1 fusion.7
  63.2 0.1 reshape.105
  63.3 0.6 fusion.4
  63.9 0.2 copy.14
  64.1 0.1 broadcast_bitcast_fusion
  64.2 0.4 reshape.106
  64.6 11.5 %all_to_all.5 = f32[8,1,5408]{2,1,0:T(1,128)S(1)} all-to-all(f32[8,1,5408]{2,1,0:T(1,128)S(1)} %reshape.106), channel_id=1, replica_groups=mesh['band'=8,'grid'=32] {'band'}, dimensions={0} | all-to-all | bytes 346112 | tf_op jit(solution)/shard_map/all_to_all | solution.py:18
  76.1 0.5 broadcast.97
  76.6 1.1 %reduce = f32[8,5408]{1,0:T(8,128)S(1)} reduce(f32[8,1,5408]{2,1,0:T(1,128)S(1)} %all_to_all.5, f32[]{:T(128)} %broadcast.97), dimensions={1}, to_apply=%all_to_all.3.reduce_sub_computation | reduce | bytes 346116 | tf_op jit(solution)/shard_map/all_to_all | solution.py:18
  77.6 0.3 reshape.107
  78.0 0.7 bitcast_reduce_fusion
  (5 shorter events, 0.0 us)
Async XLA Ops:
  12.2 8.5 %copy-start = (s32[64,8]{0,1:T(8,128)S(1)}, s32[64,8]{0,1:T(8,128)}, u32[]{:S(2)}) copy-start(s32[64,8]{0,1:T(8,128)} %param.6) | copy-start | bytes 6148
  27.2 12.9 %collective-permute-start = (f32[32,3328]{1,0:T(8,128)S(1)}, f32[32,3328]{1,0:T(8,128)S(1)}, u32[]{:S(2)}, u32[]{:S(2)}) collective-permute-start(f32[32,3328]{1,0:T(8,128)S(1)} %get-tuple-element.9), channel_id=1, source_target_pairs={{31,0},{0,1},{1,2},{2,3},{3,4},{4,5},{5,6},{6,7},{7,8},{8,9},{9,10... | collective-permute-start | bytes 1277960 | tf_op jit(solution)/shard_map/ppermute | solution.py:13
  27.3 36.0 %copy-start.1 = (f32[256]{0:T(256)S(1)}, f32[256]{0:T(256)}, u32[]{:S(2)}) copy-start(f32[256]{0:T(256)} %param.7) | copy-start | bytes 3076
  27.3 12.8 %collective-permute-start.3 = (f32[32,3328]{1,0:T(8,128)S(1)}, f32[32,3328]{1,0:T(8,128)S(1)}, u32[]{:S(2)}, u32[]{:S(2)}) collective-permute-start(f32[32,3328]{1,0:T(8,128)S(1)} %get-tuple-element.10), channel_id=1, source_target_pairs={{1,0},{2,1},{3,2},{4,3},{5,4},{6,5},{7,6},{8,7},{9,8},{10,9},{11,1... | collective-permute-start | bytes 1277960 | tf_op jit(solution)/shard_map/ppermute | solution.py:13
  40.2 11.3 %collective-permute-start.1 = (f32[32,3328]{1,0:T(8,128)S(1)}, f32[32,3328]{1,0:T(8,128)S(1)}, u32[]{:S(2)}, u32[]{:S(2)}) collective-permute-start(f32[32,3328]{1,0:T(8,128)S(1)} %get-tuple-element.7), channel_id=1, source_target_pairs={{31,0},{0,1},{1,2},{2,3},{3,4},{4,5},{5,6},{6,7},{7,8},{8,9},{9,10... | collective-permute-start | bytes 1277960 | tf_op jit(solution)/shard_map/ppermute | solution.py:13
  40.3 11.3 %collective-permute-start.4 = (f32[32,3328]{1,0:T(8,128)S(1)}, f32[32,3328]{1,0:T(8,128)S(1)}, u32[]{:S(2)}, u32[]{:S(2)}) collective-permute-start(f32[32,3328]{1,0:T(8,128)S(1)} %get-tuple-element.8), channel_id=1, source_target_pairs={{1,0},{2,1},{3,2},{4,3},{5,4},{6,5},{7,6},{8,7},{9,8},{10,9},{11,1... | collective-permute-start | bytes 1277960 | tf_op jit(solution)/shard_map/ppermute | solution.py:13
  51.7 11.3 %collective-permute-start.2 = (f32[32,3328]{1,0:T(8,128)S(1)}, f32[32,3328]{1,0:T(8,128)S(1)}, u32[]{:S(2)}, u32[]{:S(2)}) collective-permute-start(f32[32,3328]{1,0:T(8,128)S(1)} %get-tuple-element.5), channel_id=1, source_target_pairs={{31,0},{0,1},{1,2},{2,3},{3,4},{4,5},{5,6},{6,7},{7,8},{8,9},{9,10... | collective-permute-start | bytes 1277960 | tf_op jit(solution)/shard_map/ppermute | solution.py:13
  51.8 11.3 %collective-permute-start.5 = (f32[32,3328]{1,0:T(8,128)S(1)}, f32[32,3328]{1,0:T(8,128)S(1)}, u32[]{:S(2)}, u32[]{:S(2)}) collective-permute-start(f32[32,3328]{1,0:T(8,128)S(1)} %get-tuple-element.6), channel_id=1, source_target_pairs={{1,0},{2,1},{3,2},{4,3},{5,4},{6,5},{7,6},{8,7},{9,8},{10,9},{11,1... | collective-permute-start | bytes 1277960 | tf_op jit(solution)/shard_map/ppermute | solution.py:13
where the time goes:
time: 79.1 us; the launch traced here: 78.7 us
  starting transfers between devices  18.6 us (24%)
  waiting for transfers between devices  17.1 us (22%)
  matrix products  16.3 us (21%)
  local copies, waits for them, and re-layouts  13.1 us (17%)
  blocking collectives  11.5 us (15%)
  other arithmetic  2.02 us (3%)
    ppermute x6, starting transfers between devices, shifted(): return lax.ppermute(block, axis, route)  18.6 us
    ppermute x6, waiting for transfers between devices, shifted(): return lax.ppermute(block, axis, route)  17.1 us
    all_to_all x1, blocking collectives, from_everyone(): lax.all_to_all(jnp.broadcast_to(x[None], (devices, *x.shape)), axis, 0, 0...  11.5 us
    dot_general x1, matrix products, body(): jnp.einsum('ngb,gcb->gcn', grid_blocks, stacked, preferred_element_type=j...  9.37 us
    reshape x1, local copies, waits for them, and re-layouts, body(): slot_terms = slot_terms.reshape(block_count * capacity, row_len)  8.49 us
    dot_general x1, matrix products, body(): jnp.dot(selector, slot_terms, precision=lax.Precision.HIGHEST, preferred_...  6.29 us
    unnamed x9, local copies, waits for them, and re-layouts  3.65 us
  transfers between devices with their start and end apart: 6, of which 4 were waited for; matrix products, arithmetic and copies ran while one was open for 0% of the time, Pallas kernels for 0%

commit v1 on v0

v1 whole, which is shorter than its diff:
```python
import functools

import jax
import jax.numpy as jnp
from jax import lax
from jax.experimental import pallas as pl
from jax.experimental.pallas import tpu as pltpu
from jax.sharding import PartitionSpec as P

REACH = 3
ATOMS_DEV = 32
NPROJ = 13
CAP = 8
BLK = 256
CHUNK = 8
PAIRS = [(i, j) for i in range(NPROJ) for j in range(i, NPROJ)]
F32 = jnp.float32
BF16 = jnp.bfloat16


def targets(slots, domain, domains):
    half = domains // 2
    owner = slots >> 5
    rel = ((owner - domain + half) & (domains - 1)) - half
    rel = jnp.where((domain & 1) == 1, rel, -rel)
    band = jnp.where(rel < 0, -rel, jnp.where(rel > 0, rel + REACH, 0))
    return jnp.where(slots >= 0, band * ATOMS_DEV + (slots & (ATOMS_DEV - 1)), 255)


def project_kernel(
    domain_ref, slot_ref, proj_hbm, wave_hbm, own_ref, inner_ref, outer_ref, far_ref,
    wave_buf, proj_buf, hi_buf, lo_buf, wave_sem, proj_sem, *, domains,
):
    blocks = proj_hbm.shape[0]
    bands = wave_hbm.shape[0]
    chunks = blocks // CHUNK
    width = CHUNK * BLK

    def proj_copy(c):
        rows = pl.ds(c * CHUNK, CHUNK)
        return pltpu.make_async_copy(proj_hbm.at[rows], proj_buf.at[rows], proj_sem.at[c])

    def wave_copy(c):
        return pltpu.make_async_copy(
            wave_hbm.at[:, pl.ds(c * width, width)], wave_buf.at[c], wave_sem.at[c]
        )

    for c in range(chunks):
        proj_copy(c).start()
        wave_copy(c).start()

    slot_rows = targets(slot_ref[...], domain_ref[0], domains).astype(F32).astype(BF16)
    total = blocks * CAP
    spread = (
        lax.broadcasted_iota(jnp.int32, (blocks, total), 0)
        == lax.broadcasted_iota(jnp.int32, (blocks, total), 1) // CAP
    ).astype(F32).astype(BF16)
    wide = jnp.dot(slot_rows, spread, preferred_element_type=F32)
    keep = (
        lax.broadcasted_iota(jnp.int32, (CAP, total), 0)
        == lax.broadcasted_iota(jnp.int32, (CAP, total), 1) % CAP
    )
    row_of = jnp.sum(jnp.where(keep, wide, 0.0), axis=0, keepdims=True).astype(jnp.int32)

    window = (2 * REACH + 1) * ATOMS_DEV
    halves = 2
    half_slots = total // halves
    for h in range(halves):

        def one_chunk(c, carry):
            proj_copy(c).wait()
            wave_copy(c).wait()
            for q in range(CHUNK // 2):
                parts = []
                for g in (2 * q, 2 * q + 1):
                    parts.append(
                        lax.dot_general(
                            proj_buf[c * CHUNK + g],
                            wave_buf[c, :, g * BLK:(g + 1) * BLK],
                            (((1,), (1,)), ((), ())),
                            preferred_element_type=F32,
                        )
                    )
                rows = pl.ds(pl.multiple_of(c * (CHUNK * CAP) + q * 2 * CAP, 16), 2 * CAP)
                for i in range(NPROJ):
                    value = jnp.concatenate([p[i * CAP:(i + 1) * CAP] for p in parts], axis=0)
                    high = value.astype(BF16)
                    hi_buf[i, rows, :] = high
                    lo_buf[i, rows, :] = (value - high.astype(F32)).astype(BF16)
            return carry

        lax.fori_loop(h * chunks // halves, (h + 1) * chunks // halves, one_chunk, 0)
        cols = slice(h * half_slots, (h + 1) * half_slots)
        selector = (
            lax.broadcasted_iota(jnp.int32, (window, half_slots), 0) == row_of[:, cols]
        ).astype(F32).astype(BF16)
        for i in range(NPROJ):
            part = jnp.dot(selector, hi_buf[i, cols, :], preferred_element_type=F32)
            part = part + jnp.dot(selector, lo_buf[i, cols, :], preferred_element_type=F32)
            blocks_of = [part[k * ATOMS_DEV:(k + 1) * ATOMS_DEV] for k in range(2 * REACH + 1)]
            places = [(own_ref, (i,))]
            places += [(inner_ref, (k, i)) for k in range(REACH)]
            places += [(outer_ref, (k, i)) for k in range(REACH - 1)]
            places += [(far_ref, (i,))]
            for (ref, at), value in zip(places, blocks_of):
                if h == 0:
                    ref[at] = value
                else:
                    ref[at] = ref[at] + value


def project(wave, proj, slots, domain, domains):
    bands, points = wave.shape
    blocks = proj.shape[0]
    chunks = blocks // CHUNK
    block = (NPROJ, ATOMS_DEV, bands)
    vmem = pl.BlockSpec(memory_space=pltpu.VMEM)
    hbm = pl.BlockSpec(memory_space=pl.ANY)
    return pl.pallas_call(
        functools.partial(project_kernel, domains=domains),
        in_specs=[pl.BlockSpec(memory_space=pltpu.SMEM), vmem, hbm, hbm],
        out_specs=[vmem] * 4,
        out_shape=[
            jax.ShapeDtypeStruct(block, F32),
            jax.ShapeDtypeStruct((REACH,) + block, F32),
            jax.ShapeDtypeStruct((REACH - 1,) + block, F32),
            jax.ShapeDtypeStruct(block, F32),
        ],
        scratch_shapes=[
            pltpu.VMEM((chunks, bands, CHUNK * BLK), BF16),
            pltpu.VMEM((blocks, NPROJ * CAP, BLK), BF16),
            pltpu.VMEM((NPROJ, blocks * CAP, bands), BF16),
            pltpu.VMEM((NPROJ, blocks * CAP, bands), BF16),
            pltpu.SemaphoreType.DMA((chunks,)),
            pltpu.SemaphoreType.DMA((chunks,)),
        ],
        compiler_params=pltpu.CompilerParams(vmem_limit_bytes=48 * 1024 * 1024),
        name="project",
    )(domain, slots, proj, wave)


def gram_kernel(occ_ref, a_ref, b_ref, c_ref, out_ref):
    peers = out_ref.shape[0]
    occ = occ_ref[...]
    for t in range(ATOMS_DEV // 8):
        rows = slice(8 * t, 8 * t + 8)
        value = [a_ref[i, rows, :] + b_ref[i, rows, :] + c_ref[i, rows, :] for i in range(NPROJ)]
        scaled = [v * occ for v in value]
        lane = lax.broadcasted_iota(jnp.int32, (8, 128), 1)
        result = jnp.zeros((8, 128), F32)
        for p, (i, j) in enumerate(PAIRS):
            term = jnp.sum(scaled[i] * value[j], axis=1, keepdims=True)
            result = jnp.where(lane == p, term, result)
        for k in range(peers):
            out_ref[k, rows, :] = result


def gram(occ, a, b, c, peers):
    vmem = pl.BlockSpec(memory_space=pltpu.VMEM)
    return pl.pallas_call(
        gram_kernel,
        in_specs=[vmem] * 4,
        out_specs=vmem,
        out_shape=jax.ShapeDtypeStruct((peers, ATOMS_DEV, 128), F32),
        compiler_params=pltpu.CompilerParams(vmem_limit_bytes=8 * 1024 * 1024),
        name="gram",
    )(occ, a, b, c)


def unfold_kernel(in_ref, out_ref):
    total = in_ref[0]
    for k in range(1, in_ref.shape[0]):
        total = total + in_ref[k]
    padded = jnp.concatenate([total, jnp.zeros((128 - ATOMS_DEV, 128), F32)], axis=0)
    turned = jnp.transpose(padded)[:, :ATOMS_DEV]
    place = {pair: p for p, pair in enumerate(PAIRS)}
    for i in range(NPROJ):
        first = place[(i, i)]
        out_ref[i, i:NPROJ, :] = turned[first:first + NPROJ - i]
        for j in range(i + 1, NPROJ):
            out_ref[j, i:i + 1, :] = turned[first + j - i:first + j - i + 1]


def unfold(everything):
    vmem = pl.BlockSpec(memory_space=pltpu.VMEM)
    return pl.pallas_call(
        unfold_kernel,
        in_specs=[vmem],
        out_specs=vmem,
        out_shape=jax.ShapeDtypeStruct((NPROJ, NPROJ, ATOMS_DEV), F32),
        compiler_params=pltpu.CompilerParams(vmem_limit_bytes=8 * 1024 * 1024),
        name="unfold",
    )(everything)


def body(wavefunctions, projectors, slot_atom, occupations):
    band_count = wavefunctions.shape[0]
    block_count, capacity, proj_count, block_len = projectors.shape
    domains = lax.axis_size("grid")
    peers = lax.axis_size("band")
    domain = lax.axis_index("grid").astype(jnp.int32).reshape(1)
    chips = domains // 2
    stored = jnp.transpose(projectors, (0, 2, 1, 3)).reshape(
        block_count, proj_count * capacity, block_len
    )
    own, inner, outer, far = project(
        wavefunctions, stored, jnp.transpose(slot_atom), domain, domains
    )

    partner = [(i, i ^ 1) for i in range(domains)]
    along = [(2 * k + 1, (2 * k + 3) % domains) for k in range(chips)]
    along += [(2 * k, (2 * k - 2) % domains) for k in range(chips)]
    across = [(2 * k + 1, (2 * k + 2) % domains) for k in range(chips)]
    across += [(2 * k, (2 * k - 1) % domains) for k in range(chips)]

    swapped = lax.ppermute(inner, "grid", partner)
    passed = lax.ppermute(far, "grid", along)
    near = own + swapped[0]
    first = outer[0] + swapped[1]
    second = outer[1] + swapped[2]
    near, first, second = lax.optimization_barrier((near, first, second))
    final_second = lax.ppermute(second, "grid", along)
    first = first + passed
    final_first = lax.ppermute(first, "grid", across)

    occ = occupations.reshape(1, band_count)
    packed = gram(occ, near, final_second, final_first, peers)
    everything = lax.all_to_all(packed, "band", 0, 0, tiled=True)
    return jnp.transpose(unfold(everything), (2, 0, 1))


def solution(mesh):
    in_specs = (P("band", "grid"), P("grid", None, None, None), P("grid", None), P("band"))
    out_specs = P("grid", None, None)
    return jax.shard_map(body, mesh=mesh, in_specs=in_specs, out_specs=out_specs, check_vma=False)
```

time: 79.1 us -> 45 us (0.57)
  matrix products: 16.3 us -> 0 us
  local copies, waits for them, and re-layouts: 13.1 us -> 0.69 us
  Pallas kernels: 0 us -> 8.47 us
  starting transfers between devices: 18.6 us -> 12.5 us
  waiting for transfers between devices: 17.1 us -> 11.9 us
  other arithmetic: 2.02 us -> 0.29 us
    dot_general x3 -> x0, matrix products: 16.3 us -> none  [the longest x1 9.37 us: body(): jnp.einsum('ngb,gcb->gcn', grid_blocks, stacked, preferred_element_type=j...]
    reshape x3 -> x0, local copies, waits for them, and re-layouts: 8.72 us -> none  [the longest x1 8.49 us: body(): slot_terms = slot_terms.reshape(block_count * capacity, row_len)]
    pallas_call x0 -> x3, Pallas kernels: none -> 8.47 us  [the longest x1 7.23 us: project(): pl.pallas_call(functools.partial(project_kernel, domains=domains), in_spe...]
    ppermute x6 -> x4, starting transfers between devices: 18.6 us -> 12.5 us  [the longest x1 7.66 us: body(): passed = lax.ppermute(far, 'grid', along)]
    ppermute x6 -> x4, waiting for transfers between devices: 17.1 us -> 11.9 us  [the longest x1 6.75 us: body(): final_first = lax.ppermute(first, 'grid', across)]
    unnamed x9 -> x4, local copies, waits for them, and re-layouts: 3.65 us -> 0.69 us
    all_to_all x1 -> x0, other arithmetic: 1.05 us -> none  [from_everyone(): lax.all_to_all(jnp.broadcast_to(x[None], (devices, *x.shape)), axis, 0, 0...]
  transfers between devices with their start and end apart: 6 -> 4, of which waited for: 4 -> 3; matrix products, arithmetic and copies ran while one was open for 0% -> 1% of each run, Pallas kernels for 0% -> 0%
where the time goes in v1:
time: 45 us; the launch traced here: 44.9 us
  starting transfers between devices  12.5 us (28%)
  waiting for transfers between devices  11.9 us (26%)
  blocking collectives  11 us (24%)
  Pallas kernels  8.47 us (19%)
  local copies, waits for them, and re-layouts  0.69 us (2%)
    all_to_all x1, blocking collectives, body(): everything = lax.all_to_all(packed, 'band', 0, 0, tiled=True)  11 us
    ppermute x1, starting transfers between devices, body(): passed = lax.ppermute(far, 'grid', along)  7.66 us
    pallas_call x1, Pallas kernels, project(): pl.pallas_call(functools.partial(project_kernel, domains=domains), in_spe...  7.23 us
    ppermute x1, waiting for transfers between devices, body(): final_first = lax.ppermute(first, 'grid', across)  6.75 us
    ppermute x1, starting transfers between devices, body(): final_second = lax.ppermute(second, 'grid', along)  2.97 us
    ppermute x1, waiting for transfers between devices, body(): final_second = lax.ppermute(second, 'grid', along)  2.76 us
    ppermute x1, waiting for transfers between devices, body(): passed = lax.ppermute(far, 'grid', along)  2.41 us
    ppermute x1, starting transfers between devices, body(): final_first = lax.ppermute(first, 'grid', across)  1.74 us
  transfers between devices with their start and end apart: 4, of which 3 were waited for; matrix products, arithmetic and copies ran while one was open for 1% of the time, Pallas kernels for 0%

profile of v1, /device:TPU:8, one launch (start us, length us, event | category | flops | bytes accessed | tf_op | source)
XLA Modules:
  0.0 44.9 jit_solution(3275425094731480163)
XLA Ops:
  0.0 0.0 copy-start
  0.0 0.7 %copy-done = s32[64,8]{0,1:T(8,128)S(1)} copy-done((s32[64,8]{0,1:T(8,128)S(1)}, s32[64,8]{0,1:T(8,128)}, u32[]{:S(2)}) %copy-start) | copy-done | bytes 2072
  0.7 7.2 %project.1 = (f32[13,32,256]{2,1,0:T(8,128)S(1)}, f32[3,13,32,256]{3,2,1,0:T(8,128)S(1)}, f32[2,13,32,256]{3,2,1,0:T(8,128)S(1)}, f32[13,32,256]{2,1,0:T(8,128)S(1)}) custom-call(s32[1]{0:T(128)} %bitcast.1.domain_ref, s32[8,64]{1,0:T(8,128)S(1)} %bitcast.15, bf16[64,104,256]{2,1,0:T(8,128)(2,1)} %bitcast.17, bf16[256,16384]{1,0:T(8,128)(2,1)} %wave_hbm.1), custom_call_target="tpu_custom_call" | custom-call | tf_op jit(solution)/shard_map/project/pallas_call | solution.py:119
  7.9 0.1 collective-permute-start
  8.0 7.7 %collective-permute-start.2 = (f32[13,32,256]{2,1,0:T(8,128)S(1)}, f32[13,32,256]{2,1,0:T(8,128)S(1)}, u32[]{:S(2)}, u32[]{:S(2)}) collective-permute-start(f32[13,32,256]{2,1,0:T(8,128)S(1)} %get-tuple-element.18), channel_id=1, source_target_pairs={{1,3},{3,5},{5,7},{7,9},{9,11},{11,13},{13,15},{15,17},{17,19},{19... | collective-permute-start | bytes 1277960 | tf_op jit(solution)/shard_map/ppermute | solution.py:217
  15.7 0.0 collective-permute-done
  15.7 0.1 fusion.2.a_ref
  15.8 0.2 fusion
  15.9 0.0 copy-start.1
  16.0 3.0 %collective-permute-start.1 = (f32[13,32,256]{2,1,0:T(8,128)S(1)}, f32[13,32,256]{2,1,0:T(8,128)S(1)}, u32[]{:S(2)}, u32[]{:S(2)}) collective-permute-start(f32[13,32,256]{2,1,0:T(8,128)S(1)} %get-tuple-element.16), channel_id=1, source_target_pairs={{1,3},{3,5},{5,7},{7,9},{9,11},{11,13},{13,15},{15,17},{17,19},{19... | collective-permute-start | bytes 1277960 | tf_op jit(solution)/shard_map/ppermute | solution.py:222
  18.9 2.4 %collective-permute-done.2 = f32[13,32,256]{2,1,0:T(8,128)S(1)} collective-permute-done((f32[13,32,256]{2,1,0:T(8,128)S(1)}, f32[13,32,256]{2,1,0:T(8,128)S(1)}, u32[]{:S(2)}, u32[]{:S(2)}) %collective-permute-start.2) | collective-permute-done | bytes 426016 | tf_op jit(solution)/shard_map/ppermute | solution.py:217
  21.3 0.1 add.23
  21.4 1.7 %collective-permute-start.3 = (f32[13,32,256]{2,1,0:T(8,128)S(1)}, f32[13,32,256]{2,1,0:T(8,128)S(1)}, u32[]{:S(2)}, u32[]{:S(2)}) collective-permute-start(f32[13,32,256]{2,1,0:T(8,128)S(1)} %add.23), channel_id=1, source_target_pairs={{1,2},{3,4},{5,6},{7,8},{9,10},{11,12},{13,14},{15,16},{17,18},{19... | collective-permute-start | bytes 1277960 | tf_op jit(solution)/shard_map/ppermute | solution.py:224
  23.1 2.8 %collective-permute-done.1.b_ref = f32[13,32,256]{2,1,0:T(8,128)S(1)} collective-permute-done((f32[13,32,256]{2,1,0:T(8,128)S(1)}, f32[13,32,256]{2,1,0:T(8,128)S(1)}, u32[]{:S(2)}, u32[]{:S(2)}) %collective-permute-start.1) | collective-permute-done | bytes 426016 | tf_op jit(solution)/shard_map/ppermute | solution.py:222
  25.9 6.8 %collective-permute-done.3.c_ref = f32[13,32,256]{2,1,0:T(8,128)S(1)} collective-permute-done((f32[13,32,256]{2,1,0:T(8,128)S(1)}, f32[13,32,256]{2,1,0:T(8,128)S(1)}, u32[]{:S(2)}, u32[]{:S(2)}) %collective-permute-start.3) | collective-permute-done | bytes 426016 | tf_op jit(solution)/shard_map/ppermute | solution.py:224
  32.7 0.0 copy-done.1
  32.7 0.5 %gram.1 = f32[8,32,128]{2,1,0:T(8,128)S(1)} custom-call(f32[1,256]{1,0:T(1,128)S(1)} %bitcast.16, f32[13,32,256]{2,1,0:T(8,128)S(1)} %fusion.2.a_ref, f32[13,32,256]{2,1,0:T(8,128)S(1)} %collective-permute-done.1.b_ref, f32[13,32,256]{2,1,0:T(8,128)S(1)} %collective-permute-done.3.c_ref), custom_call_target="tpu_custom_call" | custom-call | tf_op jit(solution)/shard_map/gram/pallas_call | solution.py:160
  33.1 11.0 %all_to_all.5.in_ref = f32[8,32,128]{2,1,0:T(8,128)S(1)} all-to-all(f32[8,32,128]{2,1,0:T(8,128)S(1)} %gram.1), channel_id=1, replica_groups=mesh['band'=8,'grid'=32] {'band'}, dimensions={0} | all-to-all | bytes 262144 | tf_op jit(solution)/shard_map/all_to_all | solution.py:228
  44.1 0.8 %unfold.1 = f32[13,13,32]{2,1,0:T(8,128)} custom-call(f32[8,32,128]{2,1,0:T(8,128)S(1)} %all_to_all.5.in_ref), custom_call_target="tpu_custom_call" | custom-call | tf_op jit(solution)/shard_map/unfold/pallas_call | solution.py:186
Async XLA Ops:
  0.0 0.7 %copy-start = (s32[64,8]{0,1:T(8,128)S(1)}, s32[64,8]{0,1:T(8,128)}, u32[]{:S(2)}) copy-start(s32[64,8]{0,1:T(8,128)} %param.6) | copy-start | bytes 6148
  7.9 7.8 %collective-permute-start = (f32[3,13,32,256]{3,2,1,0:T(8,128)S(1)}, f32[3,13,32,256]{3,2,1,0:T(8,128)S(1)}, u32[]{:S(2)}, u32[]{:S(2)}) collective-permute-start(f32[3,13,32,256]{3,2,1,0:T(8,128)S(1)} %get-tuple-element.13), channel_id=1, source_target_pairs={{0,1},{1,0},{2,3},{3,2},{4,5},{5,4},{6,7},{7,6},{8,9},{9,8},{10,11... | collective-permute-start | bytes 3833864 | tf_op jit(solution)/shard_map/ppermute | solution.py:216
  8.0 13.3 %collective-permute-start.2 = (f32[13,32,256]{2,1,0:T(8,128)S(1)}, f32[13,32,256]{2,1,0:T(8,128)S(1)}, u32[]{:S(2)}, u32[]{:S(2)}) collective-permute-start(f32[13,32,256]{2,1,0:T(8,128)S(1)} %get-tuple-element.18), channel_id=1, source_target_pairs={{1,3},{3,5},{5,7},{7,9},{9,11},{11,13},{13,15},{15,17},{17,19},{19... | collective-permute-start | bytes 1277960 | tf_op jit(solution)/shard_map/ppermute | solution.py:217
  15.9 16.7 %copy-start.1 = (f32[256]{0:T(256)S(1)}, f32[256]{0:T(256)}, u32[]{:S(2)}) copy-start(f32[256]{0:T(256)} %param.7) | copy-start | bytes 3076
  16.0 9.9 %collective-permute-start.1 = (f32[13,32,256]{2,1,0:T(8,128)S(1)}, f32[13,32,256]{2,1,0:T(8,128)S(1)}, u32[]{:S(2)}, u32[]{:S(2)}) collective-permute-start(f32[13,32,256]{2,1,0:T(8,128)S(1)} %get-tuple-element.16), channel_id=1, source_target_pairs={{1,3},{3,5},{5,7},{7,9},{9,11},{11,13},{13,15},{15,17},{17,19},{19... | collective-permute-start | bytes 1277960 | tf_op jit(solution)/shard_map/ppermute | solution.py:222
  21.4 11.3 %collective-permute-start.3 = (f32[13,32,256]{2,1,0:T(8,128)S(1)}, f32[13,32,256]{2,1,0:T(8,128)S(1)}, u32[]{:S(2)}, u32[]{:S(2)}) collective-permute-start(f32[13,32,256]{2,1,0:T(8,128)S(1)} %add.23), channel_id=1, source_target_pairs={{1,2},{3,4},{5,6},{7,8},{9,10},{11,12},{13,14},{15,16},{17,18},{19... | collective-permute-start | bytes 1277960 | tf_op jit(solution)/shard_map/ppermute | solution.py:224

commit v2 on v1

v2 whole, which is shorter than its diff:
```python
import functools

import jax
import jax.numpy as jnp
from jax import lax
from jax.experimental import pallas as pl
from jax.experimental.pallas import tpu as pltpu
from jax.sharding import PartitionSpec as P

REACH = 3
ATOMS_DEV = 32
NPROJ = 13
CAP = 8
BLK = 256
STRIDE = 96
PAIRS = [(i, j) for i in range(NPROJ) for j in range(i, NPROJ)]
F32 = jnp.float32
BF16 = jnp.bfloat16


def targets(slots, domain, domains):
    half = domains // 2
    owner = slots >> 5
    rel = ((owner - domain + half) & (domains - 1)) - half
    rel = jnp.where((domain & 1) == 1, rel, -rel)
    band = jnp.where(rel < 0, -rel, jnp.where(rel > 0, rel + REACH, 0))
    return jnp.where(slots >= 0, band * ATOMS_DEV + (slots & (ATOMS_DEV - 1)), 255)


def project_kernel(
    domain_ref, slot_hbm, proj_hbm, wave_hbm, own_ref, inner_ref, outer_ref, far_ref,
    slot_buf, wave_buf, proj_buf, turn_buf, term_buf, slot_sem, chunk_sem, *, domains,
):
    blocks = proj_hbm.shape[0]
    total = blocks * CAP
    sizes = chunk_sizes(blocks)
    starts = [sum(sizes[:c]) for c in range(len(sizes))]
    copies = [pltpu.make_async_copy(slot_hbm, slot_buf, slot_sem)]
    for c, (first, size) in enumerate(zip(starts, sizes)):
        rows = pl.ds(first, size)
        cols = pl.ds(first * BLK, size * BLK)
        copies.append(
            pltpu.make_async_copy(proj_hbm.at[rows], proj_buf.at[rows], chunk_sem.at[c])
        )
        copies.append(
            pltpu.make_async_copy(wave_hbm.at[:, cols], wave_buf.at[:, cols], chunk_sem.at[c])
        )
    for copy in copies:
        copy.start()

    def turn(c):
        rows = sizes[c] * (NPROJ * CAP + wave_hbm.shape[0]) // 3
        both = term_buf.at[:3, :rows, :]
        pltpu.make_async_copy(both, both, chunk_sem.at[c]).wait()
        for g in range(starts[c], starts[c] + sizes[c]):
            turn_buf[g] = wave_buf[:, g * BLK:(g + 1) * BLK].T

    parts = 4
    edges = [p * total // parts for p in range(parts + 1)]

    def multiply(c):
        for g in range(starts[c], starts[c] + sizes[c], 2):
            pair = [
                jnp.dot(proj_buf[k], turn_buf[k], preferred_element_type=F32) for k in (g, g + 1)
            ]
            part = max(p for p in range(parts) if edges[p] <= g * CAP)
            size = edges[part + 1] - edges[part]
            row = edges[part] + g * CAP
            for i in range(NPROJ):
                value = jnp.concatenate([p[i * CAP:(i + 1) * CAP] for p in pair], axis=0)
                high = value.astype(BF16)
                term_buf[i, row:row + 2 * CAP, :] = high
                term_buf[i, row + size:row + size + 2 * CAP, :] = (
                    value - high.astype(F32)
                ).astype(BF16)

    window = (2 * REACH + 1) * ATOMS_DEV

    def selectors():
        copies[0].wait()
        slot_rows = targets(slot_buf[...], domain_ref[0], domains).astype(F32).astype(BF16)
        spread = (
            lax.broadcasted_iota(jnp.int32, (blocks, total), 0)
            == lax.broadcasted_iota(jnp.int32, (blocks, total), 1) // CAP
        ).astype(F32).astype(BF16)
        wide = jnp.dot(slot_rows, spread, preferred_element_type=F32)
        keep = (
            lax.broadcasted_iota(jnp.int32, (CAP, total), 0)
            == lax.broadcasted_iota(jnp.int32, (CAP, total), 1) % CAP
        )
        row_of = jnp.sum(jnp.where(keep, wide, 0.0), axis=0, keepdims=True).astype(jnp.int32)
        return row_of

    def gather(row_of, part, kinds):
        size = edges[part + 1] - edges[part]
        one = (
            lax.broadcasted_iota(jnp.int32, (window, size), 0)
            == row_of[:, edges[part]:edges[part + 1]]
        ).astype(F32).astype(BF16)
        both = jnp.concatenate([one, one], axis=1)
        for i in kinds:
            result = jnp.dot(
                both, term_buf[i, 2 * edges[part]:2 * edges[part + 1], :],
                preferred_element_type=F32,
            )
            places = [(own_ref, (i,))]
            places += [(inner_ref, (k, i)) for k in range(REACH)]
            places += [(outer_ref, (k, i)) for k in range(REACH - 1)]
            places += [(far_ref, (i,))]
            for k, (ref, at) in enumerate(places):
                value = result[k * ATOMS_DEV:(k + 1) * ATOMS_DEV]
                ref[at] = value if part == 0 else ref[at] + value

    per_part = len(sizes) // parts
    row_of = None
    for step in range(len(sizes) + 1):
        if step < len(sizes):
            turn(step)
        if step > 0:
            multiply(step - 1)
        if step == 1:
            row_of = selectors()
        ready, turn_of = divmod(step - per_part, per_part)
        if 0 <= ready < parts - 1:
            gather(row_of, ready, range(NPROJ)[turn_of::per_part])
    gather(row_of, parts - 1, range(NPROJ))


def chunk_sizes(blocks):
    return [blocks // 8] * 8


def project(wave, proj, slots, domain, domains):
    bands, points = wave.shape
    blocks = proj.shape[0]
    chunks = len(chunk_sizes(blocks))
    block = (NPROJ, ATOMS_DEV, bands)
    vmem = pl.BlockSpec(memory_space=pltpu.VMEM)
    hbm = pl.BlockSpec(memory_space=pltpu.HBM)
    return pl.pallas_call(
        functools.partial(project_kernel, domains=domains),
        in_specs=[pl.BlockSpec(memory_space=pltpu.SMEM), hbm, hbm, hbm],
        out_specs=[vmem] * 4,
        out_shape=[
            jax.ShapeDtypeStruct(block, F32),
            jax.ShapeDtypeStruct((REACH,) + block, F32),
            jax.ShapeDtypeStruct((REACH - 1,) + block, F32),
            jax.ShapeDtypeStruct(block, F32),
        ],
        scratch_shapes=[
            pltpu.VMEM(slots.shape, jnp.int32),
            pltpu.VMEM((bands, points), BF16),
            pltpu.VMEM((blocks, NPROJ * CAP, BLK), BF16),
            pltpu.VMEM((blocks, BLK, bands), BF16),
            pltpu.VMEM((NPROJ, 2 * blocks * CAP, bands), BF16),
            pltpu.SemaphoreType.DMA,
            pltpu.SemaphoreType.DMA((chunks,)),
        ],
        compiler_params=pltpu.CompilerParams(vmem_limit_bytes=48 * 1024 * 1024),
        name="project",
    )(domain, slots, proj, wave)


def gram_kernel(occ_ref, a_ref, b_ref, c_ref, out_ref):
    peers = out_ref.shape[0]
    occ = occ_ref[...]
    lane = lax.broadcasted_iota(jnp.int32, (8, 128), 1)
    packed = [jnp.zeros((8, 128), F32) for _ in range(3)]
    for t in range(ATOMS_DEV // 8):
        rows = slice(8 * t, 8 * t + 8)
        value = [a_ref[i, rows, :] + b_ref[i, rows, :] + c_ref[i, rows, :] for i in range(NPROJ)]
        scaled = [v * occ for v in value]
        for p, (i, j) in enumerate(PAIRS):
            term = jnp.sum(scaled[i] * value[j], axis=1, keepdims=True)
            word, at = divmod(STRIDE * t + p, 128)
            packed[word] = jnp.where(lane == at, term, packed[word])
    for k in range(peers):
        for word in range(3):
            out_ref[k, :, 128 * word:128 * (word + 1)] = packed[word]


def gram(occ, a, b, c, peers):
    vmem = pl.BlockSpec(memory_space=pltpu.VMEM)
    return pl.pallas_call(
        gram_kernel,
        in_specs=[vmem] * 4,
        out_specs=vmem,
        out_shape=jax.ShapeDtypeStruct((peers, 8, 3 * 128), F32),
        compiler_params=pltpu.CompilerParams(vmem_limit_bytes=8 * 1024 * 1024),
        name="gram",
    )(occ, a, b, c)


def unfold_kernel(in_ref, out_ref):
    total = in_ref[0]
    for k in range(1, in_ref.shape[0]):
        total = total + in_ref[k]
    padded = jnp.concatenate([total, jnp.zeros((120, 3 * 128), F32)], axis=0)
    turned = jnp.transpose(padded)
    turned = jnp.concatenate(
        [turned[STRIDE * t:STRIDE * (t + 1), :8] for t in range(ATOMS_DEV // 8)], axis=1
    )
    place = {pair: p for p, pair in enumerate(PAIRS)}
    for i in range(NPROJ):
        first = place[(i, i)]
        out_ref[i, i:NPROJ, :] = turned[first:first + NPROJ - i]
        for j in range(i + 1, NPROJ):
            out_ref[j, i:i + 1, :] = turned[first + j - i:first + j - i + 1]


def unfold(everything):
    vmem = pl.BlockSpec(memory_space=pltpu.VMEM)
    return pl.pallas_call(
        unfold_kernel,
        in_specs=[vmem],
        out_specs=vmem,
        out_shape=jax.ShapeDtypeStruct((NPROJ, NPROJ, ATOMS_DEV), F32),
        compiler_params=pltpu.CompilerParams(vmem_limit_bytes=8 * 1024 * 1024),
        name="unfold",
    )(everything)


def body(wavefunctions, projectors, slot_atom, occupations):
    band_count = wavefunctions.shape[0]
    block_count, capacity, proj_count, block_len = projectors.shape
    domains = lax.axis_size("grid")
    peers = lax.axis_size("band")
    domain = lax.axis_index("grid").astype(jnp.int32).reshape(1)
    chips = domains // 2
    stored = jnp.transpose(projectors, (0, 2, 1, 3)).reshape(
        block_count, proj_count * capacity, block_len
    )
    own, inner, outer, far = project(
        wavefunctions, stored, jnp.transpose(slot_atom), domain, domains
    )

    partner = [(i, i ^ 1) for i in range(domains)]
    along = [(2 * k + 1, (2 * k + 3) % domains) for k in range(chips)]
    along += [(2 * k, (2 * k - 2) % domains) for k in range(chips)]
    across = [(2 * k + 1, (2 * k + 2) % domains) for k in range(chips)]
    across += [(2 * k, (2 * k - 1) % domains) for k in range(chips)]

    swapped = lax.ppermute(inner, "grid", partner)
    passed = lax.ppermute(far, "grid", along)
    near = own + swapped[0]
    first = outer[0] + swapped[1]
    second = outer[1] + swapped[2]
    near, first, second = lax.optimization_barrier((near, first, second))
    final_second = lax.ppermute(second, "grid", along)
    first = first + passed
    final_first = lax.ppermute(first, "grid", across)

    occ = occupations.reshape(1, band_count)
    packed = gram(occ, near, final_second, final_first, peers)
    everything = lax.all_to_all(packed, "band", 0, 0, tiled=True)
    return jnp.transpose(unfold(everything), (2, 0, 1))


def solution(mesh):
    in_specs = (P("band", "grid"), P("grid", None, None, None), P("grid", None), P("band"))
    out_specs = P("grid", None, None)
    return jax.shard_map(body, mesh=mesh, in_specs=in_specs, out_specs=out_specs, check_vma=False)
```

time: 45 us -> 44.6 us (level)
  no operation moved by 1% of the time
where the time goes in v2:
time: 44.6 us; the launch traced here: 44.4 us
  starting transfers between devices  12.5 us (28%)
  waiting for transfers between devices  11.9 us (27%)
  blocking collectives  10.8 us (24%)
  Pallas kernels  8.18 us (18%)
  local copies, waits for them, and re-layouts  0.69 us (2%)
    all_to_all x1, blocking collectives, body(): everything = lax.all_to_all(packed, 'band', 0, 0, tiled=True)  10.8 us
    ppermute x1, starting transfers between devices, body(): passed = lax.ppermute(far, 'grid', along)  7.65 us
    pallas_call x1, Pallas kernels, project(): pl.pallas_call(functools.partial(project_kernel, domains=domains), in_spe...  6.81 us
    ppermute x1, waiting for transfers between devices, body(): final_first = lax.ppermute(first, 'grid', across)  6.75 us
    ppermute x1, starting transfers between devices, body(): final_second = lax.ppermute(second, 'grid', along)  2.97 us
    ppermute x1, waiting for transfers between devices, body(): final_second = lax.ppermute(second, 'grid', along)  2.76 us
    ppermute x1, waiting for transfers between devices, body(): passed = lax.ppermute(far, 'grid', along)  2.41 us
    ppermute x1, starting transfers between devices, body(): final_first = lax.ppermute(first, 'grid', across)  1.74 us
  transfers between devices with their start and end apart: 4, of which 3 were waited for; matrix products, arithmetic and copies ran while one was open for 1% of the time, Pallas kernels for 0%

profile of v2, /device:TPU:8, one launch (start us, length us, event | category | flops | bytes accessed | tf_op | source)
XLA Modules:
  0.0 44.4 jit_solution(15207986590690185954)
XLA Ops:
  0.0 0.0 copy-start
  0.0 0.7 %copy-done = s32[64,8]{0,1:T(8,128)S(1)} copy-done((s32[64,8]{0,1:T(8,128)S(1)}, s32[64,8]{0,1:T(8,128)}, u32[]{:S(2)}) %copy-start) | copy-done | bytes 2072
  0.7 6.8 %project.1 = (f32[13,32,256]{2,1,0:T(8,128)S(1)}, f32[3,13,32,256]{3,2,1,0:T(8,128)S(1)}, f32[2,13,32,256]{3,2,1,0:T(8,128)S(1)}, f32[13,32,256]{2,1,0:T(8,128)S(1)}) custom-call(s32[1]{0:T(128)} %bitcast.1.domain_ref, s32[8,64]{1,0:T(8,128)S(1)} %bitcast.15, bf16[64,104,256]{2,1,0:T(8,128)(2,1)} %bitcast.17, bf16[256,16384]{1,0:T(8,128)(2,1)} %wave_hbm.1), custom_call_target="tpu_custom_call" | custom-call | tf_op jit(solution)/shard_map/project/pallas_call | solution.py:140
  7.5 0.1 collective-permute-start
  7.6 7.7 %collective-permute-start.2 = (f32[13,32,256]{2,1,0:T(8,128)S(1)}, f32[13,32,256]{2,1,0:T(8,128)S(1)}, u32[]{:S(2)}, u32[]{:S(2)}) collective-permute-start(f32[13,32,256]{2,1,0:T(8,128)S(1)} %get-tuple-element.18), channel_id=1, source_target_pairs={{1,3},{3,5},{5,7},{7,9},{9,11},{11,13},{13,15},{15,17},{17,19},{19... | collective-permute-start | bytes 1277960 | tf_op jit(solution)/shard_map/ppermute | solution.py:244
  15.3 0.0 collective-permute-done
  15.3 0.1 fusion.2.a_ref
  15.3 0.2 fusion
  15.5 0.0 copy-start.1
  15.5 3.0 %collective-permute-start.1 = (f32[13,32,256]{2,1,0:T(8,128)S(1)}, f32[13,32,256]{2,1,0:T(8,128)S(1)}, u32[]{:S(2)}, u32[]{:S(2)}) collective-permute-start(f32[13,32,256]{2,1,0:T(8,128)S(1)} %get-tuple-element.16), channel_id=1, source_target_pairs={{1,3},{3,5},{5,7},{7,9},{9,11},{11,13},{13,15},{15,17},{17,19},{19... | collective-permute-start | bytes 1277960 | tf_op jit(solution)/shard_map/ppermute | solution.py:249
  18.5 2.4 %collective-permute-done.2 = f32[13,32,256]{2,1,0:T(8,128)S(1)} collective-permute-done((f32[13,32,256]{2,1,0:T(8,128)S(1)}, f32[13,32,256]{2,1,0:T(8,128)S(1)}, u32[]{:S(2)}, u32[]{:S(2)}) %collective-permute-start.2) | collective-permute-done | bytes 426016 | tf_op jit(solution)/shard_map/ppermute | solution.py:244
  20.9 0.1 add.23
  21.0 1.7 %collective-permute-start.3 = (f32[13,32,256]{2,1,0:T(8,128)S(1)}, f32[13,32,256]{2,1,0:T(8,128)S(1)}, u32[]{:S(2)}, u32[]{:S(2)}) collective-permute-start(f32[13,32,256]{2,1,0:T(8,128)S(1)} %add.23), channel_id=1, source_target_pairs={{1,2},{3,4},{5,6},{7,8},{9,10},{11,12},{13,14},{15,16},{17,18},{19... | collective-permute-start | bytes 1277960 | tf_op jit(solution)/shard_map/ppermute | solution.py:251
  22.7 2.8 %collective-permute-done.1.b_ref = f32[13,32,256]{2,1,0:T(8,128)S(1)} collective-permute-done((f32[13,32,256]{2,1,0:T(8,128)S(1)}, f32[13,32,256]{2,1,0:T(8,128)S(1)}, u32[]{:S(2)}, u32[]{:S(2)}) %collective-permute-start.1) | collective-permute-done | bytes 426016 | tf_op jit(solution)/shard_map/ppermute | solution.py:249
  25.5 6.8 %collective-permute-done.3.c_ref = f32[13,32,256]{2,1,0:T(8,128)S(1)} collective-permute-done((f32[13,32,256]{2,1,0:T(8,128)S(1)}, f32[13,32,256]{2,1,0:T(8,128)S(1)}, u32[]{:S(2)}, u32[]{:S(2)}) %collective-permute-start.3) | collective-permute-done | bytes 426016 | tf_op jit(solution)/shard_map/ppermute | solution.py:251
  32.2 0.0 copy-done.1
  32.2 0.5 %gram.1 = f32[8,8,384]{2,1,0:T(8,128)S(1)} custom-call(f32[1,256]{1,0:T(1,128)S(1)} %bitcast.16, f32[13,32,256]{2,1,0:T(8,128)S(1)} %fusion.2.a_ref, f32[13,32,256]{2,1,0:T(8,128)S(1)} %collective-permute-done.1.b_ref, f32[13,32,256]{2,1,0:T(8,128)S(1)} %collective-permute-done.3.c_ref), custom_call_target="tpu_custom_call" | custom-call | tf_op jit(solution)/shard_map/gram/pallas_call | solution.py:184
  32.7 10.8 %all_to_all.5.in_ref = f32[8,8,384]{2,1,0:T(8,128)S(1)} all-to-all(f32[8,8,384]{2,1,0:T(8,128)S(1)} %gram.1), channel_id=1, replica_groups=mesh['band'=8,'grid'=32] {'band'}, dimensions={0} | all-to-all | bytes 196608 | tf_op jit(solution)/shard_map/all_to_all | solution.py:255
  43.5 0.9 %unfold.1 = f32[13,13,32]{2,1,0:T(8,128)} custom-call(f32[8,8,384]{2,1,0:T(8,128)S(1)} %all_to_all.5.in_ref), custom_call_target="tpu_custom_call" | custom-call | tf_op jit(solution)/shard_map/unfold/pallas_call | solution.py:213
Async XLA Ops:
  0.0 0.7 %copy-start = (s32[64,8]{0,1:T(8,128)S(1)}, s32[64,8]{0,1:T(8,128)}, u32[]{:S(2)}) copy-start(s32[64,8]{0,1:T(8,128)} %param.6) | copy-start | bytes 6148
  7.5 7.8 %collective-permute-start = (f32[3,13,32,256]{3,2,1,0:T(8,128)S(1)}, f32[3,13,32,256]{3,2,1,0:T(8,128)S(1)}, u32[]{:S(2)}, u32[]{:S(2)}) collective-permute-start(f32[3,13,32,256]{3,2,1,0:T(8,128)S(1)} %get-tuple-element.13), channel_id=1, source_target_pairs={{0,1},{1,0},{2,3},{3,2},{4,5},{5,4},{6,7},{7,6},{8,9},{9,8},{10,11... | collective-permute-start | bytes 3833864 | tf_op jit(solution)/shard_map/ppermute | solution.py:243
  7.6 13.3 %collective-permute-start.2 = (f32[13,32,256]{2,1,0:T(8,128)S(1)}, f32[13,32,256]{2,1,0:T(8,128)S(1)}, u32[]{:S(2)}, u32[]{:S(2)}) collective-permute-start(f32[13,32,256]{2,1,0:T(8,128)S(1)} %get-tuple-element.18), channel_id=1, source_target_pairs={{1,3},{3,5},{5,7},{7,9},{9,11},{11,13},{13,15},{15,17},{17,19},{19... | collective-permute-start | bytes 1277960 | tf_op jit(solution)/shard_map/ppermute | solution.py:244
  15.5 16.7 %copy-start.1 = (f32[256]{0:T(256)S(1)}, f32[256]{0:T(256)}, u32[]{:S(2)}) copy-start(f32[256]{0:T(256)} %param.7) | copy-start | bytes 3076
  15.5 9.9 %collective-permute-start.1 = (f32[13,32,256]{2,1,0:T(8,128)S(1)}, f32[13,32,256]{2,1,0:T(8,128)S(1)}, u32[]{:S(2)}, u32[]{:S(2)}) collective-permute-start(f32[13,32,256]{2,1,0:T(8,128)S(1)} %get-tuple-element.16), channel_id=1, source_target_pairs={{1,3},{3,5},{5,7},{7,9},{9,11},{11,13},{13,15},{15,17},{17,19},{19... | collective-permute-start | bytes 1277960 | tf_op jit(solution)/shard_map/ppermute | solution.py:249
  21.0 11.3 %collective-permute-start.3 = (f32[13,32,256]{2,1,0:T(8,128)S(1)}, f32[13,32,256]{2,1,0:T(8,128)S(1)}, u32[]{:S(2)}, u32[]{:S(2)}) collective-permute-start(f32[13,32,256]{2,1,0:T(8,128)S(1)} %add.23), channel_id=1, source_target_pairs={{1,2},{3,4},{5,6},{7,8},{9,10},{11,12},{13,14},{15,16},{17,18},{19... | collective-permute-start | bytes 1277960 | tf_op jit(solution)/shard_map/ppermute | solution.py:251

commit v3 on v2

v3 whole, which is shorter than its diff:
```python
import functools

import jax
import jax.numpy as jnp
from jax import lax
from jax.experimental import pallas as pl
from jax.experimental.pallas import tpu as pltpu
from jax.sharding import PartitionSpec as P


REACH = 3
CHUNK = 8
PARTS = 4
LANES = 128
ATOMS_DEV = 32
NPROJ = 13
CAP = 8
BLK = 256
STRIDE = 96
PAIRS = [(i, j) for i in range(NPROJ) for j in range(i, NPROJ)]
F32 = jnp.float32
BF16 = jnp.bfloat16


def targets(slots, domain, domains):
    half = domains // 2
    owner = slots >> 5
    rel = ((owner - domain + half) & (domains - 1)) - half
    rel = jnp.where((domain & 1) == 1, rel, -rel)
    band = jnp.where(rel < 0, -rel, jnp.where(rel > 0, rel + REACH, 0))
    return jnp.where(slots >= 0, band * ATOMS_DEV + (slots & (ATOMS_DEV - 1)), 255)


def project_kernel(*refs, domains, start):
    domain_ref, slot_ref, proj_hbm, wave_hbm, own_ref, inner_ref, outer_ref, far_ref = refs[-13:-5]
    proj_buf, wave_buf, turn_buf, term_buf, chunk_sem = refs[-5:]
    blocks = proj_hbm.shape[0]
    total = blocks * CAP
    chunks = blocks // CHUNK
    width = CHUNK * BLK
    for c in range(chunks):
        rows = pl.ds(c * CHUNK, CHUNK)
        cols = pl.ds(c * width, width)
        pltpu.make_async_copy(proj_hbm.at[rows], proj_buf.at[rows], chunk_sem.at[c]).start()
        pltpu.make_async_copy(
            wave_hbm.at[pl.ds(start, LANES), cols], wave_buf.at[:, cols], chunk_sem.at[c]
        ).start()

    def arrive(c):
        both = term_buf.at[:2, :CHUNK * (NPROJ * CAP + LANES) // 2, :]
        pltpu.make_async_copy(both, both, chunk_sem.at[c]).wait()

    slot_rows = targets(slot_ref[...], domain_ref[0], domains).astype(F32).astype(BF16)
    spread = (
        lax.broadcasted_iota(jnp.int32, (blocks, total), 0)
        == lax.broadcasted_iota(jnp.int32, (blocks, total), 1) // CAP
    ).astype(F32).astype(BF16)
    wide = jnp.dot(slot_rows, spread, preferred_element_type=F32)
    keep = (
        lax.broadcasted_iota(jnp.int32, (CAP, total), 0)
        == lax.broadcasted_iota(jnp.int32, (CAP, total), 1) % CAP
    )
    row_of = jnp.sum(jnp.where(keep, wide, 0.0), axis=0, keepdims=True).astype(jnp.int32)

    def turn(c):
        for g in range(c * CHUNK, (c + 1) * CHUNK):
            turn_buf[g] = wave_buf[:, g * BLK:(g + 1) * BLK].T

    size = total // PARTS

    def multiply(c):
        for g in range(c * CHUNK, (c + 1) * CHUNK, 2):
            pair = [
                jnp.dot(proj_buf[k], turn_buf[k], preferred_element_type=F32) for k in (g, g + 1)
            ]
            row = g * CAP // size * size + g * CAP
            for i in range(NPROJ):
                value = jnp.concatenate([p[i * CAP:(i + 1) * CAP] for p in pair], axis=0)
                high = value.astype(BF16)
                low = (value - high.astype(F32)).astype(BF16)
                lanes = slice(i % 2 * LANES, i % 2 * LANES + LANES)
                term_buf[i // 2, row:row + 2 * CAP, lanes] = high
                term_buf[i // 2, row + size:row + size + 2 * CAP, lanes] = low

    window = (2 * REACH + 1) * ATOMS_DEV

    def gather(part, kinds):
        one = (
            lax.broadcasted_iota(jnp.int32, (window, size), 0)
            == row_of[:, part * size:(part + 1) * size]
        ).astype(F32).astype(BF16)
        both = jnp.concatenate([one, one], axis=1)
        for duo in kinds:
            result = jnp.dot(
                both, term_buf[duo, 2 * part * size:2 * (part + 1) * size, :],
                preferred_element_type=F32,
            )
            for i in range(2 * duo, min(2 * duo + 2, NPROJ)):
                places = [(own_ref, (i,))]
                places += [(inner_ref, (k, i)) for k in range(REACH)]
                places += [(outer_ref, (k, i)) for k in range(REACH - 1)]
                places += [(far_ref, (i,))]
                lanes = slice(i % 2 * LANES, i % 2 * LANES + LANES)
                for k, (ref, at) in enumerate(places):
                    value = result[k * ATOMS_DEV:(k + 1) * ATOMS_DEV, lanes]
                    ref[at] = value if part == 0 else ref[at] + value

    per_part = chunks // PARTS
    duos = range((NPROJ + 1) // 2)
    for step in range(chunks + 1):
        if step < chunks:
            arrive(step)
            turn(step)
        if step > 0:
            multiply(step - 1)
        ready, at = divmod(step - per_part, per_part)
        if 0 <= ready < PARTS - 1:
            gather(ready, duos[at::per_part])
    gather(PARTS - 1, duos)


def project(wave, proj, slots, domain, domains, start, after=()):
    points = wave.shape[1]
    blocks = proj.shape[0]
    chunks = blocks // CHUNK
    block = (NPROJ, ATOMS_DEV, LANES)
    vmem = pl.BlockSpec(memory_space=pltpu.VMEM)
    hbm = pl.BlockSpec(memory_space=pl.ANY)
    return pl.pallas_call(
        functools.partial(project_kernel, domains=domains, start=start),
        in_specs=[hbm] * len(after) + [pl.BlockSpec(memory_space=pltpu.SMEM), vmem, hbm, hbm],
        out_specs=[vmem] * 4,
        out_shape=[
            jax.ShapeDtypeStruct(block, F32),
            jax.ShapeDtypeStruct((REACH,) + block, F32),
            jax.ShapeDtypeStruct((REACH - 1,) + block, F32),
            jax.ShapeDtypeStruct(block, F32),
        ],
        scratch_shapes=[
            pltpu.VMEM((blocks, NPROJ * CAP, BLK), BF16),
            pltpu.VMEM((LANES, points), BF16),
            pltpu.VMEM((blocks, BLK, LANES), BF16),
            pltpu.VMEM(((NPROJ + 1) // 2, 2 * blocks * CAP, 2 * LANES), BF16),
            pltpu.SemaphoreType.DMA((chunks,)),
        ],
        compiler_params=pltpu.CompilerParams(vmem_limit_bytes=50 * 1024 * 1024),
        name="project",
    )(*after, domain, slots, proj, wave)


def gram_kernel(occ_ref, *refs):
    out_ref = refs[-1]
    sides = [refs[:3], refs[3:6]]
    occ = [occ_ref[:, k * LANES:(k + 1) * LANES] for k in range(2)]
    lane = lax.broadcasted_iota(jnp.int32, (8, 128), 1)
    packed = [jnp.zeros((8, 128), F32) for _ in range(3)]
    for t in range(ATOMS_DEV // 8):
        rows = slice(8 * t, 8 * t + 8)
        value = [
            [a[i, rows, :] + b[i, rows, :] + c[i, rows, :] for i in range(NPROJ)]
            for a, b, c in sides
        ]
        scaled = [[v * occ[k] for v in value[k]] for k in range(2)]
        for p, (i, j) in enumerate(PAIRS):
            term = scaled[0][i] * value[0][j] + scaled[1][i] * value[1][j]
            word, at = divmod(STRIDE * t + p, 128)
            packed[word] = jnp.where(
                lane == at, jnp.sum(term, axis=1, keepdims=True), packed[word]
            )
    for k in range(out_ref.shape[0]):
        for word in range(3):
            out_ref[k, :, 128 * word:128 * (word + 1)] = packed[word]


def gram(occ, parts, peers):
    vmem = pl.BlockSpec(memory_space=pltpu.VMEM)
    return pl.pallas_call(
        gram_kernel,
        in_specs=[vmem] * 7,
        out_specs=vmem,
        out_shape=jax.ShapeDtypeStruct((peers, 8, 3 * 128), F32),
        compiler_params=pltpu.CompilerParams(vmem_limit_bytes=8 * 1024 * 1024),
        name="gram",
    )(occ, *parts)


def unfold_kernel(in_ref, out_ref):
    total = in_ref[0]
    for k in range(1, in_ref.shape[0]):
        total = total + in_ref[k]
    padded = jnp.concatenate([total, jnp.zeros((120, 3 * 128), F32)], axis=0)
    turned = jnp.transpose(padded)
    turned = jnp.concatenate(
        [turned[STRIDE * t:STRIDE * (t + 1), :8] for t in range(ATOMS_DEV // 8)], axis=1
    )
    place = {pair: p for p, pair in enumerate(PAIRS)}
    for i in range(NPROJ):
        first = place[(i, i)]
        out_ref[i, i:NPROJ, :] = turned[first:first + NPROJ - i]
        for j in range(i + 1, NPROJ):
            out_ref[j, i:i + 1, :] = turned[first + j - i:first + j - i + 1]


def unfold(everything):
    vmem = pl.BlockSpec(memory_space=pltpu.VMEM)
    return pl.pallas_call(
        unfold_kernel,
        in_specs=[vmem],
        out_specs=vmem,
        out_shape=jax.ShapeDtypeStruct((NPROJ, NPROJ, ATOMS_DEV), F32),
        compiler_params=pltpu.CompilerParams(vmem_limit_bytes=8 * 1024 * 1024),
        name="unfold",
    )(everything)


def body(wavefunctions, projectors, slot_atom, occupations):
    band_count = wavefunctions.shape[0]
    block_count, capacity, proj_count, block_len = projectors.shape
    domains = lax.axis_size("grid")
    peers = lax.axis_size("band")
    domain = lax.axis_index("grid").astype(jnp.int32).reshape(1)
    chips = domains // 2
    stored = jnp.transpose(projectors, (0, 2, 1, 3)).reshape(
        block_count, proj_count * capacity, block_len
    )
    slots = jnp.transpose(slot_atom)

    partner = [(i, i ^ 1) for i in range(domains)]
    along = [(2 * k + 1, (2 * k + 3) % domains) for k in range(chips)]
    along += [(2 * k, (2 * k - 2) % domains) for k in range(chips)]
    across = [(2 * k + 1, (2 * k + 2) % domains) for k in range(chips)]
    across += [(2 * k, (2 * k - 1) % domains) for k in range(chips)]

    def send(own, inner, outer, far):
        swapped = lax.ppermute(inner, "grid", partner)
        passed = lax.ppermute(far, "grid", along)
        near = own + swapped[0]
        first = outer[0] + swapped[1]
        second = outer[1] + swapped[2]
        near, first, second = lax.optimization_barrier((near, first, second))
        return near, lax.ppermute(second, "grid", along), first, passed, second

    def finish(first, passed):
        return lax.ppermute(first + passed, "grid", across)

    blocks = project(wavefunctions, stored, slots, domain, domains, 0)
    near, second, first, passed, sent = send(*blocks)
    blocks = project(
        wavefunctions, stored, slots, domain, domains, LANES, (sent,)
    )
    near1, second1, first1, passed1, _ = send(*blocks)
    last = finish(first, passed)
    last1 = finish(first1, passed1)
    parts = (near, second, last, near1, second1, last1)
    packed = gram(occupations.reshape(1, band_count), parts, peers)
    everything = lax.all_to_all(packed, "band", 0, 0, tiled=True)
    return jnp.transpose(unfold(everything), (2, 0, 1))


def solution(mesh):
    in_specs = (P("band", "grid"), P("grid", None, None, None), P("grid", None), P("band"))
    out_specs = P("grid", None, None)
    return jax.shard_map(body, mesh=mesh, in_specs=in_specs, out_specs=out_specs, check_vma=False)
```

time: 44.6 us -> 55.3 us (1.24)
  starting transfers between devices: 12.5 us -> 19.2 us
  Pallas kernels: 8.18 us -> 11.6 us
  waiting for transfers between devices: 11.9 us -> 12.6 us
    ppermute x4 -> x8, starting transfers between devices: 12.5 us -> 19.2 us  [the longest x2 12.5 us: send(): passed = lax.ppermute(far, 'grid', along)]
    pallas_call x2 -> x3, Pallas kernels: 7.3 us -> 10.7 us  [the longest x2 10.2 us: project(): pl.pallas_call(functools.partial(project_kernel, domains=domains, start=s...]
    ppermute x4 -> x8, waiting for transfers between devices: 11.9 us -> 12.6 us  [the longest x2 5.51 us: send(): passed = lax.ppermute(far, 'grid', along)]
  transfers between devices with their start and end apart: 4 -> 8, of which waited for: 3 -> 4; matrix products, arithmetic and copies ran while one was open for 1% -> 0% of each run, Pallas kernels for 0% -> 0%
where the time goes in v3:
time: 55.3 us; the launch traced here: 55.2 us
  starting transfers between devices  19.2 us (35%)
  waiting for transfers between devices  12.6 us (23%)
  Pallas kernels  11.6 us (21%)
  blocking collectives  10.8 us (20%)
  local copies, waits for them, and re-layouts  0.69 us (1%)
    ppermute x2, starting transfers between devices, send(): passed = lax.ppermute(far, 'grid', along)  12.5 us
    all_to_all x1, blocking collectives, body(): everything = lax.all_to_all(packed, 'band', 0, 0, tiled=True)  10.8 us
    pallas_call x2, Pallas kernels, project(): pl.pallas_call(functools.partial(project_kernel, domains=domains, start=s...  10.2 us
    ppermute x2, waiting for transfers between devices, send(): passed = lax.ppermute(far, 'grid', along)  5.51 us
    ppermute x2, starting transfers between devices, finish(): return lax.ppermute(first + passed, 'grid', across)  5.31 us
    ppermute x2, waiting for transfers between devices, finish(): return lax.ppermute(first + passed, 'grid', across)  5.06 us
    ppermute x2, waiting for transfers between devices, send(): swapped = lax.ppermute(inner, 'grid', partner)  2.06 us
    ppermute x2, starting transfers between devices, send(): return (near, lax.ppermute(second, 'grid', along), first, passed, second)  1.11 us
  transfers between devices with their start and end apart: 8, of which 4 were waited for; matrix products, arithmetic and copies ran while one was open for 0% of the time, Pallas kernels for 0%

profile of v3, /device:TPU:8, one launch (start us, length us, event | category | flops | bytes accessed | tf_op | source)
XLA Modules:
  0.0 55.2 jit_solution(155935549718468125)
XLA Ops:
  0.0 0.0 copy-start
  0.0 0.7 %copy-done = s32[64,8]{0,1:T(8,128)S(1)} copy-done((s32[64,8]{0,1:T(8,128)S(1)}, s32[64,8]{0,1:T(8,128)}, u32[]{:S(2)}) %copy-start) | copy-done | bytes 2072
  0.7 5.1 %project.2 = (f32[13,32,128]{2,1,0:T(8,128)S(1)}, f32[3,13,32,128]{3,2,1,0:T(8,128)S(1)}, f32[2,13,32,128]{3,2,1,0:T(8,128)S(1)}, f32[13,32,128]{2,1,0:T(8,128)S(1)}) custom-call(s32[1]{0:T(128)} %bitcast.1.refs_0_.refs_1_, s32[8,64]{1,0:T(8,128)S(1)} %bitcast.23, bf16[64,104,256]{2,1,0:T(8,128)(2,1)} %bitcast.26, bf16[256,16384]{1,0:T(8,128)(2,1)} %refs_4_.1), custom_call_target="tpu_custom_call" | custom-call | tf_op jit(solution)/shard_map/project/pallas_call | solution.py:129
  5.8 0.1 collective-permute-start
  5.9 2.1 %collective-permute-done = f32[3,13,32,128]{3,2,1,0:T(8,128)S(1)} collective-permute-done((f32[3,13,32,128]{3,2,1,0:T(8,128)S(1)}, f32[3,13,32,128]{3,2,1,0:T(8,128)S(1)}, u32[]{:S(2)}, u32[]{:S(2)}) %collective-permute-start) | collective-permute-done | bytes 639008 | tf_op jit(solution)/shard_map/ppermute | solution.py:235
  8.0 0.0 copy-start.1
  8.0 0.1 fusion.3
  8.1 5.1 %project.3 = (f32[13,32,128]{2,1,0:T(8,128)S(1)}, f32[3,13,32,128]{3,2,1,0:T(8,128)S(1)}, f32[2,13,32,128]{3,2,1,0:T(8,128)S(1)}, f32[13,32,128]{2,1,0:T(8,128)S(1)}) custom-call(f32[13,32,128]{2,1,0:T(8,128)S(1)} %get-tuple-element.23.refs_0_, s32[1]{0:T(128)} %bitcast.1.refs_0_.refs_1_, s32[8,64]{1,0:T(8,128)S(1)} %bitcast.24, ...), custom_call_target="tpu_custom_call" | custom-call | tf_op jit(solution)/shard_map/project/pallas_call | solution.py:129
  13.2 0.2 collective-permute-start.4
  13.4 7.6 %collective-permute-start.2 = (f32[13,32,128]{2,1,0:T(8,128)S(1)}, f32[13,32,128]{2,1,0:T(8,128)S(1)}, u32[]{:S(2)}, u32[]{:S(2)}) collective-permute-start(f32[13,32,128]{2,1,0:T(8,128)S(1)} %get-tuple-element.25), channel_id=1, source_target_pairs={{1,3},{3,5},{5,7},{7,9},{9,11},{11,13},{13,15},{15,17},{17,19},{19... | collective-permute-start | bytes 638984 | tf_op jit(solution)/shard_map/ppermute | solution.py:236
  21.0 1.0 %collective-permute-start.1 = (f32[13,32,128]{2,1,0:T(8,128)S(1)}, f32[13,32,128]{2,1,0:T(8,128)S(1)}, u32[]{:S(2)}, u32[]{:S(2)}) collective-permute-start(f32[13,32,128]{2,1,0:T(8,128)S(1)} %get-tuple-element.23.refs_0_), channel_id=1, source_target_pairs={{1,3},{3,5},{5,7},{7,9},{9,11},{11,13},{13,15},{15,17},{17,19},{19... | collective-permute-start | bytes 638984 | tf_op jit(solution)/shard_map/ppermute | solution.py:241
  22.0 2.4 %collective-permute-done.2 = f32[13,32,128]{2,1,0:T(8,128)S(1)} collective-permute-done((f32[13,32,128]{2,1,0:T(8,128)S(1)}, f32[13,32,128]{2,1,0:T(8,128)S(1)}, u32[]{:S(2)}, u32[]{:S(2)}) %collective-permute-start.2) | collective-permute-done | bytes 213024 | tf_op jit(solution)/shard_map/ppermute | solution.py:236
  24.4 1.4 %collective-permute-start.3 = (f32[13,32,128]{2,1,0:T(8,128)S(1)}, f32[13,32,128]{2,1,0:T(8,128)S(1)}, u32[]{:S(2)}, u32[]{:S(2)}) collective-permute-start(f32[13,32,128]{2,1,0:T(8,128)S(1)} %add.41), channel_id=1, source_target_pairs={{1,2},{3,4},{5,6},{7,8},{9,10},{11,12},{13,14},{15,16},{17,18},{19... | collective-permute-start | bytes 638984 | tf_op jit(solution)/shard_map/ppermute | solution.py:244
  25.8 4.9 %collective-permute-start.6 = (f32[13,32,128]{2,1,0:T(8,128)S(1)}, f32[13,32,128]{2,1,0:T(8,128)S(1)}, u32[]{:S(2)}, u32[]{:S(2)}) collective-permute-start(f32[13,32,128]{2,1,0:T(8,128)S(1)} %get-tuple-element.32), channel_id=1, source_target_pairs={{1,3},{3,5},{5,7},{7,9},{9,11},{11,13},{13,15},{15,17},{17,19},{19... | collective-permute-start | bytes 638984 | tf_op jit(solution)/shard_map/ppermute | solution.py:236
  30.6 0.0 collective-permute-done.4
  30.6 0.1 fusion
  30.8 0.1 collective-permute-start.5
  30.9 3.2 %collective-permute-done.6 = f32[13,32,128]{2,1,0:T(8,128)S(1)} collective-permute-done((f32[13,32,128]{2,1,0:T(8,128)S(1)}, f32[13,32,128]{2,1,0:T(8,128)S(1)}, u32[]{:S(2)}, u32[]{:S(2)}) %collective-permute-start.6) | collective-permute-done | bytes 213024 | tf_op jit(solution)/shard_map/ppermute | solution.py:236
  34.0 3.9 %collective-permute-start.7 = (f32[13,32,128]{2,1,0:T(8,128)S(1)}, f32[13,32,128]{2,1,0:T(8,128)S(1)}, u32[]{:S(2)}, u32[]{:S(2)}) collective-permute-start(f32[13,32,128]{2,1,0:T(8,128)S(1)} %add.47), channel_id=1, source_target_pairs={{1,2},{3,4},{5,6},{7,8},{9,10},{11,12},{13,14},{15,16},{17,18},{19... | collective-permute-start | bytes 638984 | tf_op jit(solution)/shard_map/ppermute | solution.py:244
  37.9 0.0 collective-permute-done.3.refs_2_
  38.0 0.0 collective-permute-done.1.refs_1_
  38.0 0.0 collective-permute-done.5.refs_4_
  38.0 5.1 %collective-permute-done.7.refs_5_ = f32[13,32,128]{2,1,0:T(8,128)S(1)} collective-permute-done((f32[13,32,128]{2,1,0:T(8,128)S(1)}, f32[13,32,128]{2,1,0:T(8,128)S(1)}, u32[]{:S(2)}, u32[]{:S(2)}) %collective-permute-start.7) | collective-permute-done | bytes 213024 | tf_op jit(solution)/shard_map/ppermute | solution.py:244
  43.0 0.0 copy-done.1
  43.0 0.5 gram.1
  43.5 10.8 %all_to_all.5.in_ref = f32[8,8,384]{2,1,0:T(8,128)S(1)} all-to-all(f32[8,8,384]{2,1,0:T(8,128)S(1)} %gram.1), channel_id=1, replica_groups=mesh['band'=8,'grid'=32] {'band'}, dimensions={0} | all-to-all | bytes 196608 | tf_op jit(solution)/shard_map/all_to_all | solution.py:256
  54.3 0.9 %unfold.1 = f32[13,13,32]{2,1,0:T(8,128)} custom-call(f32[8,8,384]{2,1,0:T(8,128)S(1)} %all_to_all.5.in_ref), custom_call_target="tpu_custom_call" | custom-call | tf_op jit(solution)/shard_map/unfold/pallas_call | solution.py:206
  (4 shorter events, 0.1 us)
Async XLA Ops:
  0.0 0.7 %copy-start = (s32[64,8]{0,1:T(8,128)S(1)}, s32[64,8]{0,1:T(8,128)}, u32[]{:S(2)}) copy-start(s32[64,8]{0,1:T(8,128)} %param.6) | copy-start | bytes 6148
  5.8 2.2 %collective-permute-start = (f32[3,13,32,128]{3,2,1,0:T(8,128)S(1)}, f32[3,13,32,128]{3,2,1,0:T(8,128)S(1)}, u32[]{:S(2)}, u32[]{:S(2)}) collective-permute-start(f32[3,13,32,128]{3,2,1,0:T(8,128)S(1)} %get-tuple-element.20), channel_id=1, source_target_pairs={{0,1},{1,0},{2,3},{3,2},{4,5},{5,4},{6,7},{7,6},{8,9},{9,8},{10,11... | collective-permute-start | bytes 1916936 | tf_op jit(solution)/shard_map/ppermute | solution.py:235
  8.0 35.0 %copy-start.1 = (f32[256]{0:T(256)S(1)}, f32[256]{0:T(256)}, u32[]{:S(2)}) copy-start(f32[256]{0:T(256)} %param.7) | copy-start | bytes 3076
  13.2 17.5 %collective-permute-start.4 = (f32[3,13,32,128]{3,2,1,0:T(8,128)S(1)}, f32[3,13,32,128]{3,2,1,0:T(8,128)S(1)}, u32[]{:S(2)}, u32[]{:S(2)}) collective-permute-start(f32[3,13,32,128]{3,2,1,0:T(8,128)S(1)} %get-tuple-element.27), channel_id=1, source_target_pairs={{0,1},{1,0},{2,3},{3,2},{4,5},{5,4},{6,7},{7,6},{8,9},{9,8},{10,11... | collective-permute-start | bytes 1916936 | tf_op jit(solution)/shard_map/ppermute | solution.py:235
  13.4 11.0 %collective-permute-start.2 = (f32[13,32,128]{2,1,0:T(8,128)S(1)}, f32[13,32,128]{2,1,0:T(8,128)S(1)}, u32[]{:S(2)}, u32[]{:S(2)}) collective-permute-start(f32[13,32,128]{2,1,0:T(8,128)S(1)} %get-tuple-element.25), channel_id=1, source_target_pairs={{1,3},{3,5},{5,7},{7,9},{9,11},{11,13},{13,15},{15,17},{17,19},{19... | collective-permute-start | bytes 638984 | tf_op jit(solution)/shard_map/ppermute | solution.py:236
  21.0 17.0 %collective-permute-start.1 = (f32[13,32,128]{2,1,0:T(8,128)S(1)}, f32[13,32,128]{2,1,0:T(8,128)S(1)}, u32[]{:S(2)}, u32[]{:S(2)}) collective-permute-start(f32[13,32,128]{2,1,0:T(8,128)S(1)} %get-tuple-element.23.refs_0_), channel_id=1, source_target_pairs={{1,3},{3,5},{5,7},{7,9},{9,11},{11,13},{13,15},{15,17},{17,19},{19... | collective-permute-start | bytes 638984 | tf_op jit(solution)/shard_map/ppermute | solution.py:241
  24.4 13.6 %collective-permute-start.3 = (f32[13,32,128]{2,1,0:T(8,128)S(1)}, f32[13,32,128]{2,1,0:T(8,128)S(1)}, u32[]{:S(2)}, u32[]{:S(2)}) collective-permute-start(f32[13,32,128]{2,1,0:T(8,128)S(1)} %add.41), channel_id=1, source_target_pairs={{1,2},{3,4},{5,6},{7,8},{9,10},{11,12},{13,14},{15,16},{17,18},{19... | collective-permute-start | bytes 638984 | tf_op jit(solution)/shard_map/ppermute | solution.py:244
  25.8 8.2 %collective-permute-start.6 = (f32[13,32,128]{2,1,0:T(8,128)S(1)}, f32[13,32,128]{2,1,0:T(8,128)S(1)}, u32[]{:S(2)}, u32[]{:S(2)}) collective-permute-start(f32[13,32,128]{2,1,0:T(8,128)S(1)} %get-tuple-element.32), channel_id=1, source_target_pairs={{1,3},{3,5},{5,7},{7,9},{9,11},{11,13},{13,15},{15,17},{17,19},{19... | collective-permute-start | bytes 638984 | tf_op jit(solution)/shard_map/ppermute | solution.py:236
  30.8 7.2 %collective-permute-start.5 = (f32[13,32,128]{2,1,0:T(8,128)S(1)}, f32[13,32,128]{2,1,0:T(8,128)S(1)}, u32[]{:S(2)}, u32[]{:S(2)}) collective-permute-start(f32[13,32,128]{2,1,0:T(8,128)S(1)} %get-tuple-element.30), channel_id=1, source_target_pairs={{1,3},{3,5},{5,7},{7,9},{9,11},{11,13},{13,15},{15,17},{17,19},{19... | collective-permute-start | bytes 638984 | tf_op jit(solution)/shard_map/ppermute | solution.py:241
  34.0 9.0 %collective-permute-start.7 = (f32[13,32,128]{2,1,0:T(8,128)S(1)}, f32[13,32,128]{2,1,0:T(8,128)S(1)}, u32[]{:S(2)}, u32[]{:S(2)}) collective-permute-start(f32[13,32,128]{2,1,0:T(8,128)S(1)} %add.47), channel_id=1, source_target_pairs={{1,2},{3,4},{5,6},{7,8},{9,10},{11,12},{13,14},{15,16},{17,18},{19... | collective-permute-start | bytes 638984 | tf_op jit(solution)/shard_map/ppermute | solution.py:244

commit v4 on v2

--- a/solution.py
+++ b/solution.py
@@ -45,8 +45,9 @@
         copies.append(
             pltpu.make_async_copy(wave_hbm.at[:, cols], wave_buf.at[:, cols], chunk_sem.at[c])
         )
-    for copy in copies:
-        copy.start()
+    copies[0].start()
+    for copy in copies[1:]:
+        copy.start(priority=1)
 
     def turn(c):
         rows = sizes[c] * (NPROJ * CAP + wave_hbm.shape[0]) // 3
@@ -137,6 +138,7 @@
     block = (NPROJ, ATOMS_DEV, bands)
     vmem = pl.BlockSpec(memory_space=pltpu.VMEM)
     hbm = pl.BlockSpec(memory_space=pltpu.HBM)
+    slots = pltpu.with_memory_space_constraint(slots, pltpu.HBM)
     return pl.pallas_call(
         functools.partial(project_kernel, domains=domains),
         in_specs=[pl.BlockSpec(memory_space=pltpu.SMEM), hbm, hbm, hbm],

time: 44.6 us -> 43.8 us (0.982)
  local copies, waits for them, and re-layouts: 0.69 us -> 0.01 us
    unnamed x4 -> x2, local copies, waits for them, and re-layouts: 0.69 us -> 0.01 us
where the time goes in v4:
time: 43.8 us; the launch traced here: 43.7 us
  starting transfers between devices  12.5 us (29%)
  waiting for transfers between devices  12 us (27%)
  blocking collectives  10.8 us (25%)
  Pallas kernels  8.17 us (19%)
    all_to_all x1, blocking collectives, body(): everything = lax.all_to_all(packed, 'band', 0, 0, tiled=True)  10.8 us
    ppermute x1, starting transfers between devices, body(): passed = lax.ppermute(far, 'grid', along)  7.66 us
    pallas_call x1, Pallas kernels, project(): pl.pallas_call(functools.partial(project_kernel, domains=domains), in_spe...  6.81 us
    ppermute x1, waiting for transfers between devices, body(): final_first = lax.ppermute(first, 'grid', across)  6.75 us
    ppermute x1, starting transfers between devices, body(): final_second = lax.ppermute(second, 'grid', along)  2.97 us
    ppermute x1, waiting for transfers between devices, body(): final_second = lax.ppermute(second, 'grid', along)  2.76 us
    ppermute x1, waiting for transfers between devices, body(): passed = lax.ppermute(far, 'grid', along)  2.47 us
    ppermute x1, starting transfers between devices, body(): final_first = lax.ppermute(first, 'grid', across)  1.74 us
  transfers between devices with their start and end apart: 4, of which 3 were waited for; matrix products, arithmetic and copies ran while one was open for 1% of the time, Pallas kernels for 0%

profile of v4, /device:TPU:8, one launch (start us, length us, event | category | flops | bytes accessed | tf_op | source)
XLA Modules:
  0.0 43.7 jit_solution(14981877455597627325)
XLA Ops:
  0.0 6.8 %project.1 = (f32[13,32,256]{2,1,0:T(8,128)S(1)}, f32[3,13,32,256]{3,2,1,0:T(8,128)S(1)}, f32[2,13,32,256]{3,2,1,0:T(8,128)S(1)}, f32[13,32,256]{2,1,0:T(8,128)S(1)}) custom-call(s32[1]{0:T(128)} %bitcast.1.domain_ref, s32[8,64]{1,0:T(8,128)} %bitcast.17, bf16[64,104,256]{2,1,0:T(8,128)(2,1)} %bitcast.16, bf16[256,16384]{1,0:T(8,128)(2,1)} %wave_hbm.1), custom_call_target="tpu_custom_call" | custom-call | tf_op jit(solution)/shard_map/project/pallas_call | solution.py:142
  6.8 0.1 collective-permute-start
  6.9 7.7 %collective-permute-start.2 = (f32[13,32,256]{2,1,0:T(8,128)S(1)}, f32[13,32,256]{2,1,0:T(8,128)S(1)}, u32[]{:S(2)}, u32[]{:S(2)}) collective-permute-start(f32[13,32,256]{2,1,0:T(8,128)S(1)} %get-tuple-element.18), channel_id=1, source_target_pairs={{1,3},{3,5},{5,7},{7,9},{9,11},{11,13},{13,15},{15,17},{17,19},{19... | collective-permute-start | bytes 1277960 | tf_op jit(solution)/shard_map/ppermute | solution.py:246
  14.6 0.0 collective-permute-done
  14.6 0.1 fusion.2.a_ref
  14.7 0.1 fusion
  14.8 0.0 copy-start
  14.8 3.0 %collective-permute-start.1 = (f32[13,32,256]{2,1,0:T(8,128)S(1)}, f32[13,32,256]{2,1,0:T(8,128)S(1)}, u32[]{:S(2)}, u32[]{:S(2)}) collective-permute-start(f32[13,32,256]{2,1,0:T(8,128)S(1)} %get-tuple-element.16), channel_id=1, source_target_pairs={{1,3},{3,5},{5,7},{7,9},{9,11},{11,13},{13,15},{15,17},{17,19},{19... | collective-permute-start | bytes 1277960 | tf_op jit(solution)/shard_map/ppermute | solution.py:251
  17.8 2.5 %collective-permute-done.2 = f32[13,32,256]{2,1,0:T(8,128)S(1)} collective-permute-done((f32[13,32,256]{2,1,0:T(8,128)S(1)}, f32[13,32,256]{2,1,0:T(8,128)S(1)}, u32[]{:S(2)}, u32[]{:S(2)}) %collective-permute-start.2) | collective-permute-done | bytes 426016 | tf_op jit(solution)/shard_map/ppermute | solution.py:246
  20.2 0.1 add.23
  20.3 1.7 %collective-permute-start.3 = (f32[13,32,256]{2,1,0:T(8,128)S(1)}, f32[13,32,256]{2,1,0:T(8,128)S(1)}, u32[]{:S(2)}, u32[]{:S(2)}) collective-permute-start(f32[13,32,256]{2,1,0:T(8,128)S(1)} %add.23), channel_id=1, source_target_pairs={{1,2},{3,4},{5,6},{7,8},{9,10},{11,12},{13,14},{15,16},{17,18},{19... | collective-permute-start | bytes 1277960 | tf_op jit(solution)/shard_map/ppermute | solution.py:253
  22.0 2.8 %collective-permute-done.1.b_ref = f32[13,32,256]{2,1,0:T(8,128)S(1)} collective-permute-done((f32[13,32,256]{2,1,0:T(8,128)S(1)}, f32[13,32,256]{2,1,0:T(8,128)S(1)}, u32[]{:S(2)}, u32[]{:S(2)}) %collective-permute-start.1) | collective-permute-done | bytes 426016 | tf_op jit(solution)/shard_map/ppermute | solution.py:251
  24.8 6.8 %collective-permute-done.3.c_ref = f32[13,32,256]{2,1,0:T(8,128)S(1)} collective-permute-done((f32[13,32,256]{2,1,0:T(8,128)S(1)}, f32[13,32,256]{2,1,0:T(8,128)S(1)}, u32[]{:S(2)}, u32[]{:S(2)}) %collective-permute-start.3) | collective-permute-done | bytes 426016 | tf_op jit(solution)/shard_map/ppermute | solution.py:253
  31.5 0.0 copy-done
  31.6 0.5 %gram.1 = f32[8,8,384]{2,1,0:T(8,128)S(1)} custom-call(f32[1,256]{1,0:T(1,128)S(1)} %bitcast.15, f32[13,32,256]{2,1,0:T(8,128)S(1)} %fusion.2.a_ref, f32[13,32,256]{2,1,0:T(8,128)S(1)} %collective-permute-done.1.b_ref, f32[13,32,256]{2,1,0:T(8,128)S(1)} %collective-permute-done.3.c_ref), custom_call_target="tpu_custom_call" | custom-call | tf_op jit(solution)/shard_map/gram/pallas_call | solution.py:186
  32.0 10.8 %all_to_all.5.in_ref = f32[8,8,384]{2,1,0:T(8,128)S(1)} all-to-all(f32[8,8,384]{2,1,0:T(8,128)S(1)} %gram.1), channel_id=1, replica_groups=mesh['band'=8,'grid'=32] {'band'}, dimensions={0} | all-to-all | bytes 196608 | tf_op jit(solution)/shard_map/all_to_all | solution.py:257
  42.8 0.9 %unfold.1 = f32[13,13,32]{2,1,0:T(8,128)} custom-call(f32[8,8,384]{2,1,0:T(8,128)S(1)} %all_to_all.5.in_ref), custom_call_target="tpu_custom_call" | custom-call | tf_op jit(solution)/shard_map/unfold/pallas_call | solution.py:215
Async XLA Ops:
  6.8 7.8 %collective-permute-start = (f32[3,13,32,256]{3,2,1,0:T(8,128)S(1)}, f32[3,13,32,256]{3,2,1,0:T(8,128)S(1)}, u32[]{:S(2)}, u32[]{:S(2)}) collective-permute-start(f32[3,13,32,256]{3,2,1,0:T(8,128)S(1)} %get-tuple-element.13), channel_id=1, source_target_pairs={{0,1},{1,0},{2,3},{3,2},{4,5},{5,4},{6,7},{7,6},{8,9},{9,8},{10,11... | collective-permute-start | bytes 3833864 | tf_op jit(solution)/shard_map/ppermute | solution.py:245
  6.9 13.3 %collective-permute-start.2 = (f32[13,32,256]{2,1,0:T(8,128)S(1)}, f32[13,32,256]{2,1,0:T(8,128)S(1)}, u32[]{:S(2)}, u32[]{:S(2)}) collective-permute-start(f32[13,32,256]{2,1,0:T(8,128)S(1)} %get-tuple-element.18), channel_id=1, source_target_pairs={{1,3},{3,5},{5,7},{7,9},{9,11},{11,13},{13,15},{15,17},{17,19},{19... | collective-permute-start | bytes 1277960 | tf_op jit(solution)/shard_map/ppermute | solution.py:246
  14.8 16.8 %copy-start = (f32[256]{0:T(256)S(1)}, f32[256]{0:T(256)}, u32[]{:S(2)}) copy-start(f32[256]{0:T(256)} %param.7) | copy-start | bytes 3076
  14.8 10.0 %collective-permute-start.1 = (f32[13,32,256]{2,1,0:T(8,128)S(1)}, f32[13,32,256]{2,1,0:T(8,128)S(1)}, u32[]{:S(2)}, u32[]{:S(2)}) collective-permute-start(f32[13,32,256]{2,1,0:T(8,128)S(1)} %get-tuple-element.16), channel_id=1, source_target_pairs={{1,3},{3,5},{5,7},{7,9},{9,11},{11,13},{13,15},{15,17},{17,19},{19... | collective-permute-start | bytes 1277960 | tf_op jit(solution)/shard_map/ppermute | solution.py:251
  20.3 11.3 %collective-permute-start.3 = (f32[13,32,256]{2,1,0:T(8,128)S(1)}, f32[13,32,256]{2,1,0:T(8,128)S(1)}, u32[]{:S(2)}, u32[]{:S(2)}) collective-permute-start(f32[13,32,256]{2,1,0:T(8,128)S(1)} %add.23), channel_id=1, source_target_pairs={{1,2},{3,4},{5,6},{7,8},{9,10},{11,12},{13,14},{15,16},{17,18},{19... | collective-permute-start | bytes 1277960 | tf_op jit(solution)/shard_map/ppermute | solution.py:253

commit v5 on v4

--- a/solution.py
+++ b/solution.py
@@ -49,18 +49,20 @@
     for copy in copies[1:]:
         copy.start(priority=1)
 
-    def turn(c):
+    def arrive(c):
         rows = sizes[c] * (NPROJ * CAP + wave_hbm.shape[0]) // 3
         both = term_buf.at[:3, :rows, :]
         pltpu.make_async_copy(both, both, chunk_sem.at[c]).wait()
-        for g in range(starts[c], starts[c] + sizes[c]):
+
+    def turn(c, q):
+        for g in range(starts[c] + 2 * q, starts[c] + 2 * q + 2):
             turn_buf[g] = wave_buf[:, g * BLK:(g + 1) * BLK].T
 
     parts = 4
     edges = [p * total // parts for p in range(parts + 1)]
 
-    def multiply(c):
-        for g in range(starts[c], starts[c] + sizes[c], 2):
+    def multiply(c, q):
+        for g in range(starts[c] + 2 * q, starts[c] + 2 * q + 2, 2):
             pair = [
                 jnp.dot(proj_buf[k], turn_buf[k], preferred_element_type=F32) for k in (g, g + 1)
             ]
@@ -116,14 +118,19 @@
     row_of = None
     for step in range(len(sizes) + 1):
         if step < len(sizes):
-            turn(step)
-        if step > 0:
-            multiply(step - 1)
+            arrive(step)
         if step == 1:
             row_of = selectors()
-        ready, turn_of = divmod(step - per_part, per_part)
-        if 0 <= ready < parts - 1:
-            gather(row_of, ready, range(NPROJ)[turn_of::per_part])
+        ready, turn_of = divmod(step - per_part - 1, per_part)
+        kinds = list(range(NPROJ))[turn_of::per_part] if 0 <= ready < parts - 1 else []
+        count = sizes[0] // 2
+        for q in range(count):
+            if step > 0:
+                multiply(step - 1, q)
+            if kinds[q::count]:
+                gather(row_of, ready, kinds[q::count])
+            if step < len(sizes):
+                turn(step, q)
     gather(row_of, parts - 1, range(NPROJ))
 
 

time: 43.8 us -> 43.5 us (level)
  no operation moved by 1% of the time
where the time goes in v5:
time: 43.5 us; the launch traced here: 43.4 us
  starting transfers between devices  12.5 us (29%)
  waiting for transfers between devices  12 us (28%)
  blocking collectives  10.8 us (25%)
  Pallas kernels  7.84 us (18%)
    all_to_all x1, blocking collectives, body(): everything = lax.all_to_all(packed, 'band', 0, 0, tiled=True)  10.8 us
    ppermute x1, starting transfers between devices, body(): passed = lax.ppermute(far, 'grid', along)  7.66 us
    ppermute x1, waiting for transfers between devices, body(): final_first = lax.ppermute(first, 'grid', across)  6.75 us
    pallas_call x1, Pallas kernels, project(): pl.pallas_call(functools.partial(project_kernel, domains=domains), in_spe...  6.48 us
    ppermute x1, starting transfers between devices, body(): final_second = lax.ppermute(second, 'grid', along)  2.97 us
    ppermute x1, waiting for transfers between devices, body(): final_second = lax.ppermute(second, 'grid', along)  2.76 us
    ppermute x1, waiting for transfers between devices, body(): passed = lax.ppermute(far, 'grid', along)  2.47 us
    ppermute x1, starting transfers between devices, body(): final_first = lax.ppermute(first, 'grid', across)  1.74 us
  transfers between devices with their start and end apart: 4, of which 3 were waited for; matrix products, arithmetic and copies ran while one was open for 1% of the time, Pallas kernels for 0%

profile of v5, /device:TPU:8, one launch (start us, length us, event | category | flops | bytes accessed | tf_op | source)
XLA Modules:
  0.0 43.4 jit_solution(13747465650923427809)
XLA Ops:
  0.0 6.5 %project.1 = (f32[13,32,256]{2,1,0:T(8,128)S(1)}, f32[3,13,32,256]{3,2,1,0:T(8,128)S(1)}, f32[2,13,32,256]{3,2,1,0:T(8,128)S(1)}, f32[13,32,256]{2,1,0:T(8,128)S(1)}) custom-call(s32[1]{0:T(128)} %bitcast.1.domain_ref, s32[8,64]{1,0:T(8,128)} %bitcast.17, bf16[64,104,256]{2,1,0:T(8,128)(2,1)} %bitcast.16, bf16[256,16384]{1,0:T(8,128)(2,1)} %wave_hbm.1), custom_call_target="tpu_custom_call" | custom-call | tf_op jit(solution)/shard_map/project/pallas_call | solution.py:149
  6.5 0.1 collective-permute-start
  6.6 7.7 %collective-permute-start.2 = (f32[13,32,256]{2,1,0:T(8,128)S(1)}, f32[13,32,256]{2,1,0:T(8,128)S(1)}, u32[]{:S(2)}, u32[]{:S(2)}) collective-permute-start(f32[13,32,256]{2,1,0:T(8,128)S(1)} %get-tuple-element.18), channel_id=1, source_target_pairs={{1,3},{3,5},{5,7},{7,9},{9,11},{11,13},{13,15},{15,17},{17,19},{19... | collective-permute-start | bytes 1277960 | tf_op jit(solution)/shard_map/ppermute | solution.py:253
  14.2 0.0 collective-permute-done
  14.3 0.1 fusion.2.a_ref
  14.3 0.1 fusion
  14.4 0.0 copy-start
  14.5 3.0 %collective-permute-start.1 = (f32[13,32,256]{2,1,0:T(8,128)S(1)}, f32[13,32,256]{2,1,0:T(8,128)S(1)}, u32[]{:S(2)}, u32[]{:S(2)}) collective-permute-start(f32[13,32,256]{2,1,0:T(8,128)S(1)} %get-tuple-element.16), channel_id=1, source_target_pairs={{1,3},{3,5},{5,7},{7,9},{9,11},{11,13},{13,15},{15,17},{17,19},{19... | collective-permute-start | bytes 1277960 | tf_op jit(solution)/shard_map/ppermute | solution.py:258
  17.4 2.5 %collective-permute-done.2 = f32[13,32,256]{2,1,0:T(8,128)S(1)} collective-permute-done((f32[13,32,256]{2,1,0:T(8,128)S(1)}, f32[13,32,256]{2,1,0:T(8,128)S(1)}, u32[]{:S(2)}, u32[]{:S(2)}) %collective-permute-start.2) | collective-permute-done | bytes 426016 | tf_op jit(solution)/shard_map/ppermute | solution.py:253
  19.9 0.1 add.23
  20.0 1.7 %collective-permute-start.3 = (f32[13,32,256]{2,1,0:T(8,128)S(1)}, f32[13,32,256]{2,1,0:T(8,128)S(1)}, u32[]{:S(2)}, u32[]{:S(2)}) collective-permute-start(f32[13,32,256]{2,1,0:T(8,128)S(1)} %add.23), channel_id=1, source_target_pairs={{1,2},{3,4},{5,6},{7,8},{9,10},{11,12},{13,14},{15,16},{17,18},{19... | collective-permute-start | bytes 1277960 | tf_op jit(solution)/shard_map/ppermute | solution.py:260
  21.7 2.8 %collective-permute-done.1.b_ref = f32[13,32,256]{2,1,0:T(8,128)S(1)} collective-permute-done((f32[13,32,256]{2,1,0:T(8,128)S(1)}, f32[13,32,256]{2,1,0:T(8,128)S(1)}, u32[]{:S(2)}, u32[]{:S(2)}) %collective-permute-start.1) | collective-permute-done | bytes 426016 | tf_op jit(solution)/shard_map/ppermute | solution.py:258
  24.5 6.8 %collective-permute-done.3.c_ref = f32[13,32,256]{2,1,0:T(8,128)S(1)} collective-permute-done((f32[13,32,256]{2,1,0:T(8,128)S(1)}, f32[13,32,256]{2,1,0:T(8,128)S(1)}, u32[]{:S(2)}, u32[]{:S(2)}) %collective-permute-start.3) | collective-permute-done | bytes 426016 | tf_op jit(solution)/shard_map/ppermute | solution.py:260
  31.2 0.0 copy-done
  31.2 0.5 %gram.1 = f32[8,8,384]{2,1,0:T(8,128)S(1)} custom-call(f32[1,256]{1,0:T(1,128)S(1)} %bitcast.15, f32[13,32,256]{2,1,0:T(8,128)S(1)} %fusion.2.a_ref, f32[13,32,256]{2,1,0:T(8,128)S(1)} %collective-permute-done.1.b_ref, f32[13,32,256]{2,1,0:T(8,128)S(1)} %collective-permute-done.3.c_ref), custom_call_target="tpu_custom_call" | custom-call | tf_op jit(solution)/shard_map/gram/pallas_call | solution.py:193
  31.7 10.8 %all_to_all.5.in_ref = f32[8,8,384]{2,1,0:T(8,128)S(1)} all-to-all(f32[8,8,384]{2,1,0:T(8,128)S(1)} %gram.1), channel_id=1, replica_groups=mesh['band'=8,'grid'=32] {'band'}, dimensions={0} | all-to-all | bytes 196608 | tf_op jit(solution)/shard_map/all_to_all | solution.py:264
  42.5 0.9 %unfold.1 = f32[13,13,32]{2,1,0:T(8,128)} custom-call(f32[8,8,384]{2,1,0:T(8,128)S(1)} %all_to_all.5.in_ref), custom_call_target="tpu_custom_call" | custom-call | tf_op jit(solution)/shard_map/unfold/pallas_call | solution.py:222
Async XLA Ops:
  6.5 7.8 %collective-permute-start = (f32[3,13,32,256]{3,2,1,0:T(8,128)S(1)}, f32[3,13,32,256]{3,2,1,0:T(8,128)S(1)}, u32[]{:S(2)}, u32[]{:S(2)}) collective-permute-start(f32[3,13,32,256]{3,2,1,0:T(8,128)S(1)} %get-tuple-element.13), channel_id=1, source_target_pairs={{0,1},{1,0},{2,3},{3,2},{4,5},{5,4},{6,7},{7,6},{8,9},{9,8},{10,11... | collective-permute-start | bytes 3833864 | tf_op jit(solution)/shard_map/ppermute | solution.py:252
  6.6 13.3 %collective-permute-start.2 = (f32[13,32,256]{2,1,0:T(8,128)S(1)}, f32[13,32,256]{2,1,0:T(8,128)S(1)}, u32[]{:S(2)}, u32[]{:S(2)}) collective-permute-start(f32[13,32,256]{2,1,0:T(8,128)S(1)} %get-tuple-element.18), channel_id=1, source_target_pairs={{1,3},{3,5},{5,7},{7,9},{9,11},{11,13},{13,15},{15,17},{17,19},{19... | collective-permute-start | bytes 1277960 | tf_op jit(solution)/shard_map/ppermute | solution.py:253
  14.4 16.8 %copy-start = (f32[256]{0:T(256)S(1)}, f32[256]{0:T(256)}, u32[]{:S(2)}) copy-start(f32[256]{0:T(256)} %param.7) | copy-start | bytes 3076
  14.5 10.0 %collective-permute-start.1 = (f32[13,32,256]{2,1,0:T(8,128)S(1)}, f32[13,32,256]{2,1,0:T(8,128)S(1)}, u32[]{:S(2)}, u32[]{:S(2)}) collective-permute-start(f32[13,32,256]{2,1,0:T(8,128)S(1)} %get-tuple-element.16), channel_id=1, source_target_pairs={{1,3},{3,5},{5,7},{7,9},{9,11},{11,13},{13,15},{15,17},{17,19},{19... | collective-permute-start | bytes 1277960 | tf_op jit(solution)/shard_map/ppermute | solution.py:258
  20.0 11.3 %collective-permute-start.3 = (f32[13,32,256]{2,1,0:T(8,128)S(1)}, f32[13,32,256]{2,1,0:T(8,128)S(1)}, u32[]{:S(2)}, u32[]{:S(2)}) collective-permute-start(f32[13,32,256]{2,1,0:T(8,128)S(1)} %add.23), channel_id=1, source_target_pairs={{1,2},{3,4},{5,6},{7,8},{9,10},{11,12},{13,14},{15,16},{17,18},{19... | collective-permute-start | bytes 1277960 | tf_op jit(solution)/shard_map/ppermute | solution.py:260

commit v6 on v5

--- a/solution.py
+++ b/solution.py
@@ -36,22 +36,29 @@
     sizes = chunk_sizes(blocks)
     starts = [sum(sizes[:c]) for c in range(len(sizes))]
     copies = [pltpu.make_async_copy(slot_hbm, slot_buf, slot_sem)]
-    for c, (first, size) in enumerate(zip(starts, sizes)):
-        rows = pl.ds(first, size)
-        cols = pl.ds(first * BLK, size * BLK)
-        copies.append(
-            pltpu.make_async_copy(proj_hbm.at[rows], proj_buf.at[rows], chunk_sem.at[c])
-        )
+    arriving = []
+    for c in range(len(sizes)):
+        cols = pl.ds(starts[c] * BLK, sizes[c] * BLK)
+        kept = [c - 1] if c else []
+        kept += [c] if c == len(sizes) - 1 else []
+        for k in kept:
+            rows = pl.ds(starts[k], sizes[k])
+            copies.append(
+                pltpu.make_async_copy(proj_hbm.at[rows], proj_buf.at[rows], chunk_sem.at[c])
+            )
         copies.append(
             pltpu.make_async_copy(wave_hbm.at[:, cols], wave_buf.at[:, cols], chunk_sem.at[c])
+        )
+        arriving.append(
+            sizes[c] * wave_hbm.shape[0] + sum(sizes[k] for k in kept) * NPROJ * CAP
         )
     copies[0].start()
     for copy in copies[1:]:
         copy.start(priority=1)
 
     def arrive(c):
-        rows = sizes[c] * (NPROJ * CAP + wave_hbm.shape[0]) // 3
-        both = term_buf.at[:3, :rows, :]
+        deep = 4 if arriving[c] % 64 == 0 else 3
+        both = term_buf.at[:deep, :arriving[c] // deep, :]
         pltpu.make_async_copy(both, both, chunk_sem.at[c]).wait()
 
     def turn(c, q):

time: 43.5 us -> 43.4 us (level)
  no operation moved by 1% of the time
where the time goes in v6:
time: 43.4 us; the launch traced here: 43.2 us
  starting transfers between devices  12.5 us (29%)
  waiting for transfers between devices  12 us (28%)
  blocking collectives  10.8 us (25%)
  Pallas kernels  7.71 us (18%)
    all_to_all x1, blocking collectives, body(): everything = lax.all_to_all(packed, 'band', 0, 0, tiled=True)  10.8 us
    ppermute x1, starting transfers between devices, body(): passed = lax.ppermute(far, 'grid', along)  7.67 us
    ppermute x1, waiting for transfers between devices, body(): final_first = lax.ppermute(first, 'grid', across)  6.75 us
    pallas_call x1, Pallas kernels, project(): pl.pallas_call(functools.partial(project_kernel, domains=domains), in_spe...  6.34 us
    ppermute x1, starting transfers between devices, body(): final_second = lax.ppermute(second, 'grid', along)  2.97 us
    ppermute x1, waiting for transfers between devices, body(): final_second = lax.ppermute(second, 'grid', along)  2.76 us
    ppermute x1, waiting for transfers between devices, body(): passed = lax.ppermute(far, 'grid', along)  2.47 us
    ppermute x1, starting transfers between devices, body(): final_first = lax.ppermute(first, 'grid', across)  1.74 us
  transfers between devices with their start and end apart: 4, of which 3 were waited for; matrix products, arithmetic and copies ran while one was open for 1% of the time, Pallas kernels for 0%

profile of v6, /device:TPU:8, one launch (start us, length us, event | category | flops | bytes accessed | tf_op | source)
XLA Modules:
  0.0 43.2 jit_solution(5445879985779041277)
XLA Ops:
  0.0 6.3 %project.1 = (f32[13,32,256]{2,1,0:T(8,128)S(1)}, f32[3,13,32,256]{3,2,1,0:T(8,128)S(1)}, f32[2,13,32,256]{3,2,1,0:T(8,128)S(1)}, f32[13,32,256]{2,1,0:T(8,128)S(1)}) custom-call(s32[1]{0:T(128)} %bitcast.1.domain_ref, s32[8,64]{1,0:T(8,128)} %bitcast.17, bf16[64,104,256]{2,1,0:T(8,128)(2,1)} %bitcast.16, bf16[256,16384]{1,0:T(8,128)(2,1)} %wave_hbm.1), custom_call_target="tpu_custom_call" | custom-call | tf_op jit(solution)/shard_map/project/pallas_call | solution.py:156
  6.4 0.1 collective-permute-start
  6.5 7.7 %collective-permute-start.2 = (f32[13,32,256]{2,1,0:T(8,128)S(1)}, f32[13,32,256]{2,1,0:T(8,128)S(1)}, u32[]{:S(2)}, u32[]{:S(2)}) collective-permute-start(f32[13,32,256]{2,1,0:T(8,128)S(1)} %get-tuple-element.18), channel_id=1, source_target_pairs={{1,3},{3,5},{5,7},{7,9},{9,11},{11,13},{13,15},{15,17},{17,19},{19... | collective-permute-start | bytes 1277960 | tf_op jit(solution)/shard_map/ppermute | solution.py:260
  14.1 0.0 collective-permute-done
  14.1 0.1 fusion.2.a_ref
  14.2 0.1 fusion
  14.3 0.0 copy-start
  14.3 3.0 %collective-permute-start.1 = (f32[13,32,256]{2,1,0:T(8,128)S(1)}, f32[13,32,256]{2,1,0:T(8,128)S(1)}, u32[]{:S(2)}, u32[]{:S(2)}) collective-permute-start(f32[13,32,256]{2,1,0:T(8,128)S(1)} %get-tuple-element.16), channel_id=1, source_target_pairs={{1,3},{3,5},{5,7},{7,9},{9,11},{11,13},{13,15},{15,17},{17,19},{19... | collective-permute-start | bytes 1277960 | tf_op jit(solution)/shard_map/ppermute | solution.py:265
  17.3 2.5 %collective-permute-done.2 = f32[13,32,256]{2,1,0:T(8,128)S(1)} collective-permute-done((f32[13,32,256]{2,1,0:T(8,128)S(1)}, f32[13,32,256]{2,1,0:T(8,128)S(1)}, u32[]{:S(2)}, u32[]{:S(2)}) %collective-permute-start.2) | collective-permute-done | bytes 426016 | tf_op jit(solution)/shard_map/ppermute | solution.py:260
  19.8 0.1 add.23
  19.8 1.7 %collective-permute-start.3 = (f32[13,32,256]{2,1,0:T(8,128)S(1)}, f32[13,32,256]{2,1,0:T(8,128)S(1)}, u32[]{:S(2)}, u32[]{:S(2)}) collective-permute-start(f32[13,32,256]{2,1,0:T(8,128)S(1)} %add.23), channel_id=1, source_target_pairs={{1,2},{3,4},{5,6},{7,8},{9,10},{11,12},{13,14},{15,16},{17,18},{19... | collective-permute-start | bytes 1277960 | tf_op jit(solution)/shard_map/ppermute | solution.py:267
  21.6 2.8 %collective-permute-done.1.b_ref = f32[13,32,256]{2,1,0:T(8,128)S(1)} collective-permute-done((f32[13,32,256]{2,1,0:T(8,128)S(1)}, f32[13,32,256]{2,1,0:T(8,128)S(1)}, u32[]{:S(2)}, u32[]{:S(2)}) %collective-permute-start.1) | collective-permute-done | bytes 426016 | tf_op jit(solution)/shard_map/ppermute | solution.py:265
  24.3 6.8 %collective-permute-done.3.c_ref = f32[13,32,256]{2,1,0:T(8,128)S(1)} collective-permute-done((f32[13,32,256]{2,1,0:T(8,128)S(1)}, f32[13,32,256]{2,1,0:T(8,128)S(1)}, u32[]{:S(2)}, u32[]{:S(2)}) %collective-permute-start.3) | collective-permute-done | bytes 426016 | tf_op jit(solution)/shard_map/ppermute | solution.py:267
  31.1 0.0 copy-done
  31.1 0.5 %gram.1 = f32[8,8,384]{2,1,0:T(8,128)S(1)} custom-call(f32[1,256]{1,0:T(1,128)S(1)} %bitcast.15, f32[13,32,256]{2,1,0:T(8,128)S(1)} %fusion.2.a_ref, f32[13,32,256]{2,1,0:T(8,128)S(1)} %collective-permute-done.1.b_ref, f32[13,32,256]{2,1,0:T(8,128)S(1)} %collective-permute-done.3.c_ref), custom_call_target="tpu_custom_call" | custom-call | tf_op jit(solution)/shard_map/gram/pallas_call | solution.py:200
  31.6 10.8 %all_to_all.5.in_ref = f32[8,8,384]{2,1,0:T(8,128)S(1)} all-to-all(f32[8,8,384]{2,1,0:T(8,128)S(1)} %gram.1), channel_id=1, replica_groups=mesh['band'=8,'grid'=32] {'band'}, dimensions={0} | all-to-all | bytes 196608 | tf_op jit(solution)/shard_map/all_to_all | solution.py:271
  42.4 0.9 %unfold.1 = f32[13,13,32]{2,1,0:T(8,128)} custom-call(f32[8,8,384]{2,1,0:T(8,128)S(1)} %all_to_all.5.in_ref), custom_call_target="tpu_custom_call" | custom-call | tf_op jit(solution)/shard_map/unfold/pallas_call | solution.py:229
Async XLA Ops:
  6.4 7.8 %collective-permute-start = (f32[3,13,32,256]{3,2,1,0:T(8,128)S(1)}, f32[3,13,32,256]{3,2,1,0:T(8,128)S(1)}, u32[]{:S(2)}, u32[]{:S(2)}) collective-permute-start(f32[3,13,32,256]{3,2,1,0:T(8,128)S(1)} %get-tuple-element.13), channel_id=1, source_target_pairs={{0,1},{1,0},{2,3},{3,2},{4,5},{5,4},{6,7},{7,6},{8,9},{9,8},{10,11... | collective-permute-start | bytes 3833864 | tf_op jit(solution)/shard_map/ppermute | solution.py:259
  6.5 13.3 %collective-permute-start.2 = (f32[13,32,256]{2,1,0:T(8,128)S(1)}, f32[13,32,256]{2,1,0:T(8,128)S(1)}, u32[]{:S(2)}, u32[]{:S(2)}) collective-permute-start(f32[13,32,256]{2,1,0:T(8,128)S(1)} %get-tuple-element.18), channel_id=1, source_target_pairs={{1,3},{3,5},{5,7},{7,9},{9,11},{11,13},{13,15},{15,17},{17,19},{19... | collective-permute-start | bytes 1277960 | tf_op jit(solution)/shard_map/ppermute | solution.py:260
  14.3 16.8 %copy-start = (f32[256]{0:T(256)S(1)}, f32[256]{0:T(256)}, u32[]{:S(2)}) copy-start(f32[256]{0:T(256)} %param.7) | copy-start | bytes 3076
  14.3 10.0 %collective-permute-start.1 = (f32[13,32,256]{2,1,0:T(8,128)S(1)}, f32[13,32,256]{2,1,0:T(8,128)S(1)}, u32[]{:S(2)}, u32[]{:S(2)}) collective-permute-start(f32[13,32,256]{2,1,0:T(8,128)S(1)} %get-tuple-element.16), channel_id=1, source_target_pairs={{1,3},{3,5},{5,7},{7,9},{9,11},{11,13},{13,15},{15,17},{17,19},{19... | collective-permute-start | bytes 1277960 | tf_op jit(solution)/shard_map/ppermute | solution.py:265
  19.8 11.3 %collective-permute-start.3 = (f32[13,32,256]{2,1,0:T(8,128)S(1)}, f32[13,32,256]{2,1,0:T(8,128)S(1)}, u32[]{:S(2)}, u32[]{:S(2)}) collective-permute-start(f32[13,32,256]{2,1,0:T(8,128)S(1)} %add.23), channel_id=1, source_target_pairs={{1,2},{3,4},{5,6},{7,8},{9,10},{11,12},{13,14},{15,16},{17,18},{19... | collective-permute-start | bytes 1277960 | tf_op jit(solution)/shard_map/ppermute | solution.py:267
